TPU v7x, 32 devices: a 4x4x1 block of a 4x4x8 slice. The times are simulated.
32 devices in a mesh: data: 1 (over z), col: 4 (over y), row: 8 (over x, core).
Axes of the slice: x: 4, y: 4, z: 1, core: 2. Of those that a mesh axis runs over, the one named last changes fastest.
The devices are a block of a 4x4x8 slice.
Arguments:
- pair_rep: bfloat16 [512, 512, 64], P(('data', 'row'), 'col')
- res_mask: int32 [512], P('data')
- ln_gamma: float32 [64], replicated
- ln_beta: float32 [64], replicated
- w_q: bfloat16 [64, 64], replicated
- w_k: bfloat16 [64, 64], replicated
- w_v: bfloat16 [64, 64], replicated
- w_b: bfloat16 [64, 4], replicated
- w_g: bfloat16 [64, 64], replicated
- w_o: bfloat16 [64, 64], replicated
Outputs:
- output: bfloat16 [512, 512, 64], P(('data', 'row'), 'col')
All inputs are finite; a program needn't handle non-finite values.
Results may differ from a plain program's by a relative error of at most 0.00619686.
Values are sent between devices in bfloat16 or wider.
A program may use at most 768 MiB of HBM per device.

v0:
```python
import math
import jax
import jax.numpy as jnp
from jax import lax
from jax.sharding import PartitionSpec as P

LN_EPS = 1e-5
MASK_FILL = -1e9


def norm_and_project(pair_tile, ln_gamma, ln_beta, w_q, w_k, w_v, w_b, w_g):
    n_chan = pair_tile.shape[-1]
    heads = w_b.shape[1]
    head_dim = w_q.shape[1] // heads
    pair_f32 = pair_tile.astype(jnp.float32)
    mean = jnp.mean(pair_f32, axis=-1, keepdims=True)
    centred = pair_f32 - mean
    variance = jnp.mean(centred * centred, axis=-1, keepdims=True)
    normed = (centred * lax.rsqrt(variance + LN_EPS) * ln_gamma + ln_beta).astype(jnp.bfloat16)
    query = (jnp.einsum('ijc,chd->jhid', normed, w_q.reshape(n_chan, heads, head_dim), preferred_element_type=jnp.float32) * (1.0 / math.sqrt(head_dim))).astype(jnp.bfloat16)
    w_kv = jnp.stack([w_k.reshape(n_chan, heads, head_dim), w_v.reshape(n_chan, heads, head_dim)])
    kv_pair = jnp.einsum('ijc,echd->ejhid', normed, w_kv, preferred_element_type=jnp.float32).astype(jnp.bfloat16)
    gate = jax.nn.sigmoid(jnp.einsum('ijc,chd->jhid', normed, w_g.reshape(n_chan, heads, head_dim), preferred_element_type=jnp.float32))
    bias_tile = jnp.einsum('ijc,ch->ijh', normed, w_b, preferred_element_type=jnp.float32).astype(jnp.bfloat16)
    return pair_f32, query, kv_pair, gate, bias_tile


def bias_strip(bias_tile):
    full_cols = lax.all_gather(bias_tile, 'col', axis=1, tiled=True)
    own_rows = lax.all_to_all(full_cols, 'row', 1, 0, tiled=True)
    return jnp.transpose(own_rows, (2, 1, 0))


def attend_block(state, query, kv_blk, bias_blk, fill_blk):
    run_max, run_sum, out_acc = state
    logits = jnp.einsum('jhid,jhkd->jhik', query, kv_blk[0], preferred_element_type=jnp.float32) + bias_blk[None] + fill_blk
    new_max = jnp.maximum(run_max, jnp.max(logits, axis=-1))
    rescale = jnp.exp(run_max - new_max)
    p_exp = jnp.exp(logits - new_max[..., None])
    run_sum = run_sum * rescale + jnp.sum(p_exp, axis=-1)
    out_acc = out_acc * rescale[..., None] + jnp.einsum('jhik,jhkd->jhid', p_exp.astype(jnp.bfloat16), kv_blk[1], preferred_element_type=jnp.float32)
    return new_max, run_sum, out_acc


def finish(state, gate, pair_f32, w_o):
    run_max, run_sum, out_acc = state
    heads = gate.shape[1]
    head_dim = gate.shape[3]
    gated = (gate * (out_acc / run_sum[..., None])).astype(jnp.bfloat16)
    update = jnp.einsum('jhid,hdc->ijc', gated, w_o.reshape(heads, head_dim, w_o.shape[1]), preferred_element_type=jnp.float32)
    return (pair_f32 + update).astype(jnp.bfloat16)


def solution(mesh):
    rows = mesh.shape['row']
    next_hop = [(src_id, (src_id + 1) % rows) for src_id in range(rows)]

    def body(pair_tile, res_mask, ln_gamma, ln_beta, w_q, w_k, w_v, w_b, w_g, w_o):
        pair_f32, query, kv_pair, gate, bias_tile = norm_and_project(pair_tile, ln_gamma, ln_beta, w_q, w_k, w_v, w_b, w_g)
        strip = bias_strip(bias_tile)
        key_fill = jnp.where(res_mask > 0, 0.0, MASK_FILL).astype(jnp.float32)
        block = pair_tile.shape[0]
        my_row = lax.axis_index('row')

        def fold(step, state, kv_blk):
            key_lo = ((my_row - step) % rows) * block
            bias_blk = lax.dynamic_slice_in_dim(strip, key_lo, block, axis=2)
            fill_blk = lax.dynamic_slice_in_dim(key_fill, key_lo, block)
            return attend_block(state, query, kv_blk, bias_blk, fill_blk)

        stat_shape = query.shape[:3]
        state = (jnp.full(stat_shape, -jnp.inf, jnp.float32), jnp.zeros(stat_shape, jnp.float32), jnp.zeros(query.shape, jnp.float32))
        state = fold(0, state, kv_pair)

        def shift_step(step, carry):
            cur_state, kv_blk = carry
            kv_blk = lax.ppermute(kv_blk, 'row', next_hop)
            return fold(step, cur_state, kv_blk), kv_blk

        state, kv_last = lax.fori_loop(1, rows, shift_step, (state, kv_pair))
        return finish(state, gate, pair_f32, w_o)

    tile_spec = P(('data', 'row'), 'col', None)
    return jax.shard_map(body, mesh=mesh, in_specs=(tile_spec, P('data'), P(), P(), P(), P(), P(), P(), P(), P()), out_specs=tile_spec, check_vma=False)
```

profile of v0, /device:TPU:96, one launch (start us, length us, event | category | flops | bytes accessed | tf_op | source)
XLA Modules:
  0.0 636.7 jit_solution(5056772338554077866)
XLA Ops:
  0.0 1.6 convert_reduce_fusion
  1.6 1.6 fusion.26
  3.3 1.8 fusion.29
  5.4 12.4 %all_gather.3 = bf16[64,512,4]{1,2,0:T(4,128)(2,1)S(1)} all-gather(bf16[64,128,4]{1,2,0:T(4,128)(2,1)S(1)} %convolution_convert_fusion), channel_id=1, replica_groups=mesh['data'=1,'col'=4,'row'=8] {'col'}, dimensions={1}, use_global_device_ids=true | all-gather | bytes 327680 | tf_op jit(solution)/shard_map/all_gather | solution.py:29
  19.3 4.6 all-to-all-start
  29.5 4.3 copy.61
  33.8 3.5 copy.60
  37.3 5.4 copy.65
  42.7 4.9 copy.69
  50.7 11.1 %fusion.15 = (f32[128,4,64]{2,1,0:T(4,128)S(1)}, f32[128,4,64,64]{2,3,1,0:T(8,128)}) fusion(f32[64]{0:T(128)S(1)} %dynamic_slice.27, f32[4,64,64]{1,2,0:T(8,128)S(1)} %convert_bitcast_fusion.1, bf16[128,4,64,16]{2,3,1,0:T(8,128)(2,1)S(1)} %copy.60, bf16[128,4,64,16]{2,3,1,0:T(8,128)(2,1)} %copy.61), kind=kOutput, calls=%fused_computation.18 | convolution fusion | flops 73367552 | bytes 10682624 | tf_op jit(solution)/shard_map/jhid,jhkd->jhik/dot_general | solution.py:36
  61.8 11.4 %fusion.17 = f32[128,4,64]{2,1,0:T(4,128)S(1)} fusion(f32[128,4,64,64]{2,3,1,0:T(8,128)} %get-tuple-element.294, f32[128,4,64]{2,1,0:T(4,128)S(1)} %get-tuple-element.367, f32[64]{0:T(128)S(1)} %dynamic_slice.27, f32[4,64,64]{1,2,0:T(8,128)S(1)} %convert_bitcast_fusion.1), kind=kLoop, calls=%fused_computation.20 | loop fusion | flops 8355840 | bytes 8716544 | tf_op jit(solution)/shard_map/reduce_sum | solution.py:40
  74.1 11.7 %broadcast_add_fusion = f32[128,4,64,16]{2,3,1,0:T(8,128)} fusion(f32[128,4,64]{2,1,0:T(4,128)S(1)} %get-tuple-element.291, bf16[128,4,64,16]{2,3,1,0:T(8,128)(2,1)} %copy.65, f32[128,4,64,64]{2,3,1,0:T(8,128)} %get-tuple-element.294, f32[128,4,64]{2,1,0:T(4,128)S(1)} %get-tuple-element.367, f32[64]{0:T(128)S(1)} %dynamic_slice.27, ...), kind=kOutput, calls=%fused_computation.37 | convolution fusion | flops 76021760 | bytes 11862272 | tf_op jit(solution)/shard_map/jhik,jhkd->jhid/dot_general | solution.py:41
  85.8 538.1 %while.21 = (s32[]{:T(128)}, f32[128,4,64]{2,1,0:T(4,128)S(1)}, f32[128,4,64]{2,1,0:T(4,128)}, f32[128,4,64,16]{2,3,1,0:T(8,128)}, bf16[2,128,4,64,16]{1,4,3,2,0...) while((s32[]{:T(128)}, f32[128,4,64]{2,1,0:T(4,128)S(1)}, ...), condition=%wide.region_7.8_spmd, body=%wide.region_4.7_spmd.sunk | while | flops 158416912 | bytes 82102088 | solution.py:80
  89.3 24.7 %collective-permute-done = bf16[2,128,4,64,16]{1,4,3,2,0:T(8,128)(2,1)S(1)} collective-permute-done((bf16[2,128,4,64,16]{1,4,3,2,0:T(8,128)(2,1)}, bf16[2,128,4,64,16]{1,4,3,2,0:T(8,128)(2,1)S(1)}, u32[]{:S(2)}, u32[]{:S(2)}) %collective-permute-start) | collective-permute-done | bytes 2097184 | tf_op jit(solution)/shard_map/while/body/eval_jaxpr/ppermute | solution.py:77
  114.0 1.6 fusion.62
  115.6 5.4 copy.81
  120.9 3.3 copy.82
  124.2 11.7 %fusion.63 = (f32[128,4,64]{2,1,0:T(4,128)S(1)}, f32[128,4,64,64]{2,3,1,0:T(8,128)}) fusion(f32[64]{0:T(128)} %dynamic_slice.33, f32[4,64,64]{1,2,0:T(8,128)S(1)} %dynamic-slice_convert_fusion.2, bf16[128,4,64,16]{2,3,1,0:T(8,128)(2,1)} %copy-done.3, bf16[1,128,4,64,16]{3,4,2,1,0:T(8,128)(2,1)} %copy.81), kind=kOutput, calls=%fused_computation.2.clone.1 | convolution fusion | flops 73367552 | bytes 10682624 | tf_op jit(solution)/shard_map/while/body/eval_jaxpr/jhid,jhkd->jhik/dot_general | solution.py:36
  136.0 11.5 %fusion.64 = f32[128,4,64]{2,1,0:T(4,128)S(1)} fusion(f32[128,4,64,64]{2,3,1,0:T(8,128)} %get-tuple-element.362, f32[128,4,64]{2,1,0:T(4,128)S(1)} %max.11, f32[64]{0:T(128)} %dynamic_slice.33, f32[4,64,64]{1,2,0:T(8,128)S(1)} %dynamic-slice_convert_fusion.2), kind=kLoop, calls=%fused_computation.4.clone.1 | loop fusion | flops 8355840 | bytes 8716544 | tf_op jit(solution)/shard_map/while/body/eval_jaxpr/reduce_sum | solution.py:40
  147.8 12.5 %multiply_add_fusion.5 = f32[128,4,64,16]{2,3,1,0:T(8,128)} fusion(f32[128,4,64,16]{2,3,1,0:T(8,128)} %get-tuple-element.384, f32[128,4,64]{2,1,0:T(4,128)S(1)} %bitcast.105, f32[128,4,64,64]{2,3,1,0:T(8,128)} %get-tuple-element.362, f32[128,4,64]{2,1,0:T(4,128)S(1)} %max.11, f32[64]{0:T(128)} %dynamic_slice.33, ...), kind=kOutput, calls=%fused_computation.9.clone.1 | convolution fusion | flops 76546048 | bytes 13959424 | tf_op jit(solution)/shard_map/while/body/eval_jaxpr/jhik,jhkd->jhid/dot_general | solution.py:41
  165.6 25.2 %collective-permute-done = bf16[2,128,4,64,16]{1,4,3,2,0:T(8,128)(2,1)S(1)} collective-permute-done((bf16[2,128,4,64,16]{1,4,3,2,0:T(8,128)(2,1)}, bf16[2,128,4,64,16]{1,4,3,2,0:T(8,128)(2,1)S(1)}, u32[]{:S(2)}, u32[]{:S(2)}) %collective-permute-start) | collective-permute-done | bytes 2097184 | tf_op jit(solution)/shard_map/while/body/eval_jaxpr/ppermute | solution.py:77
  190.8 1.6 fusion.62
  192.4 5.4 copy.81
  197.7 3.3 copy.82
  201.0 11.7 %fusion.63 = (f32[128,4,64]{2,1,0:T(4,128)S(1)}, f32[128,4,64,64]{2,3,1,0:T(8,128)}) fusion(f32[64]{0:T(128)} %dynamic_slice.33, f32[4,64,64]{1,2,0:T(8,128)S(1)} %dynamic-slice_convert_fusion.2, bf16[128,4,64,16]{2,3,1,0:T(8,128)(2,1)} %copy-done.3, bf16[1,128,4,64,16]{3,4,2,1,0:T(8,128)(2,1)} %copy.81), kind=kOutput, calls=%fused_computation.2.clone.1 | convolution fusion | flops 73367552 | bytes 10682624 | tf_op jit(solution)/shard_map/while/body/eval_jaxpr/jhid,jhkd->jhik/dot_general | solution.py:36
  212.8 11.5 %fusion.64 = f32[128,4,64]{2,1,0:T(4,128)S(1)} fusion(f32[128,4,64,64]{2,3,1,0:T(8,128)} %get-tuple-element.362, f32[128,4,64]{2,1,0:T(4,128)S(1)} %max.11, f32[64]{0:T(128)} %dynamic_slice.33, f32[4,64,64]{1,2,0:T(8,128)S(1)} %dynamic-slice_convert_fusion.2), kind=kLoop, calls=%fused_computation.4.clone.1 | loop fusion | flops 8355840 | bytes 8716544 | tf_op jit(solution)/shard_map/while/body/eval_jaxpr/reduce_sum | solution.py:40
  224.7 12.5 %multiply_add_fusion.5 = f32[128,4,64,16]{2,3,1,0:T(8,128)} fusion(f32[128,4,64,16]{2,3,1,0:T(8,128)} %get-tuple-element.384, f32[128,4,64]{2,1,0:T(4,128)S(1)} %bitcast.105, f32[128,4,64,64]{2,3,1,0:T(8,128)} %get-tuple-element.362, f32[128,4,64]{2,1,0:T(4,128)S(1)} %max.11, f32[64]{0:T(128)} %dynamic_slice.33, ...), kind=kOutput, calls=%fused_computation.9.clone.1 | convolution fusion | flops 76546048 | bytes 13959424 | tf_op jit(solution)/shard_map/while/body/eval_jaxpr/jhik,jhkd->jhid/dot_general | solution.py:41
  242.4 25.2 %collective-permute-done = bf16[2,128,4,64,16]{1,4,3,2,0:T(8,128)(2,1)S(1)} collective-permute-done((bf16[2,128,4,64,16]{1,4,3,2,0:T(8,128)(2,1)}, bf16[2,128,4,64,16]{1,4,3,2,0:T(8,128)(2,1)S(1)}, u32[]{:S(2)}, u32[]{:S(2)}) %collective-permute-start) | collective-permute-done | bytes 2097184 | tf_op jit(solution)/shard_map/while/body/eval_jaxpr/ppermute | solution.py:77
  267.6 1.6 fusion.62
  269.2 5.4 copy.81
  274.6 3.3 copy.82
  277.8 11.7 %fusion.63 = (f32[128,4,64]{2,1,0:T(4,128)S(1)}, f32[128,4,64,64]{2,3,1,0:T(8,128)}) fusion(f32[64]{0:T(128)} %dynamic_slice.33, f32[4,64,64]{1,2,0:T(8,128)S(1)} %dynamic-slice_convert_fusion.2, bf16[128,4,64,16]{2,3,1,0:T(8,128)(2,1)} %copy-done.3, bf16[1,128,4,64,16]{3,4,2,1,0:T(8,128)(2,1)} %copy.81), kind=kOutput, calls=%fused_computation.2.clone.1 | convolution fusion | flops 73367552 | bytes 10682624 | tf_op jit(solution)/shard_map/while/body/eval_jaxpr/jhid,jhkd->jhik/dot_general | solution.py:36
  289.6 11.5 %fusion.64 = f32[128,4,64]{2,1,0:T(4,128)S(1)} fusion(f32[128,4,64,64]{2,3,1,0:T(8,128)} %get-tuple-element.362, f32[128,4,64]{2,1,0:T(4,128)S(1)} %max.11, f32[64]{0:T(128)} %dynamic_slice.33, f32[4,64,64]{1,2,0:T(8,128)S(1)} %dynamic-slice_convert_fusion.2), kind=kLoop, calls=%fused_computation.4.clone.1 | loop fusion | flops 8355840 | bytes 8716544 | tf_op jit(solution)/shard_map/while/body/eval_jaxpr/reduce_sum | solution.py:40
  301.5 12.5 %multiply_add_fusion.5 = f32[128,4,64,16]{2,3,1,0:T(8,128)} fusion(f32[128,4,64,16]{2,3,1,0:T(8,128)} %get-tuple-element.384, f32[128,4,64]{2,1,0:T(4,128)S(1)} %bitcast.105, f32[128,4,64,64]{2,3,1,0:T(8,128)} %get-tuple-element.362, f32[128,4,64]{2,1,0:T(4,128)S(1)} %max.11, f32[64]{0:T(128)} %dynamic_slice.33, ...), kind=kOutput, calls=%fused_computation.9.clone.1 | convolution fusion | flops 76546048 | bytes 13959424 | tf_op jit(solution)/shard_map/while/body/eval_jaxpr/jhik,jhkd->jhid/dot_general | solution.py:41
  319.2 25.2 %collective-permute-done = bf16[2,128,4,64,16]{1,4,3,2,0:T(8,128)(2,1)S(1)} collective-permute-done((bf16[2,128,4,64,16]{1,4,3,2,0:T(8,128)(2,1)}, bf16[2,128,4,64,16]{1,4,3,2,0:T(8,128)(2,1)S(1)}, u32[]{:S(2)}, u32[]{:S(2)}) %collective-permute-start) | collective-permute-done | bytes 2097184 | tf_op jit(solution)/shard_map/while/body/eval_jaxpr/ppermute | solution.py:77
  344.4 1.6 fusion.62
  346.0 5.4 copy.81
  351.4 3.3 copy.82
  354.6 11.7 %fusion.63 = (f32[128,4,64]{2,1,0:T(4,128)S(1)}, f32[128,4,64,64]{2,3,1,0:T(8,128)}) fusion(f32[64]{0:T(128)} %dynamic_slice.33, f32[4,64,64]{1,2,0:T(8,128)S(1)} %dynamic-slice_convert_fusion.2, bf16[128,4,64,16]{2,3,1,0:T(8,128)(2,1)} %copy-done.3, bf16[1,128,4,64,16]{3,4,2,1,0:T(8,128)(2,1)} %copy.81), kind=kOutput, calls=%fused_computation.2.clone.1 | convolution fusion | flops 73367552 | bytes 10682624 | tf_op jit(solution)/shard_map/while/body/eval_jaxpr/jhid,jhkd->jhik/dot_general | solution.py:36
  366.5 11.5 %fusion.64 = f32[128,4,64]{2,1,0:T(4,128)S(1)} fusion(f32[128,4,64,64]{2,3,1,0:T(8,128)} %get-tuple-element.362, f32[128,4,64]{2,1,0:T(4,128)S(1)} %max.11, f32[64]{0:T(128)} %dynamic_slice.33, f32[4,64,64]{1,2,0:T(8,128)S(1)} %dynamic-slice_convert_fusion.2), kind=kLoop, calls=%fused_computation.4.clone.1 | loop fusion | flops 8355840 | bytes 8716544 | tf_op jit(solution)/shard_map/while/body/eval_jaxpr/reduce_sum | solution.py:40
  378.3 12.5 %multiply_add_fusion.5 = f32[128,4,64,16]{2,3,1,0:T(8,128)} fusion(f32[128,4,64,16]{2,3,1,0:T(8,128)} %get-tuple-element.384, f32[128,4,64]{2,1,0:T(4,128)S(1)} %bitcast.105, f32[128,4,64,64]{2,3,1,0:T(8,128)} %get-tuple-element.362, f32[128,4,64]{2,1,0:T(4,128)S(1)} %max.11, f32[64]{0:T(128)} %dynamic_slice.33, ...), kind=kOutput, calls=%fused_computation.9.clone.1 | convolution fusion | flops 76546048 | bytes 13959424 | tf_op jit(solution)/shard_map/while/body/eval_jaxpr/jhik,jhkd->jhid/dot_general | solution.py:41
  396.0 25.2 %collective-permute-done = bf16[2,128,4,64,16]{1,4,3,2,0:T(8,128)(2,1)S(1)} collective-permute-done((bf16[2,128,4,64,16]{1,4,3,2,0:T(8,128)(2,1)}, bf16[2,128,4,64,16]{1,4,3,2,0:T(8,128)(2,1)S(1)}, u32[]{:S(2)}, u32[]{:S(2)}) %collective-permute-start) | collective-permute-done | bytes 2097184 | tf_op jit(solution)/shard_map/while/body/eval_jaxpr/ppermute | solution.py:77
  421.2 1.6 fusion.62
  422.8 5.4 copy.81
  428.2 3.3 copy.82
  431.4 11.7 %fusion.63 = (f32[128,4,64]{2,1,0:T(4,128)S(1)}, f32[128,4,64,64]{2,3,1,0:T(8,128)}) fusion(f32[64]{0:T(128)} %dynamic_slice.33, f32[4,64,64]{1,2,0:T(8,128)S(1)} %dynamic-slice_convert_fusion.2, bf16[128,4,64,16]{2,3,1,0:T(8,128)(2,1)} %copy-done.3, bf16[1,128,4,64,16]{3,4,2,1,0:T(8,128)(2,1)} %copy.81), kind=kOutput, calls=%fused_computation.2.clone.1 | convolution fusion | flops 73367552 | bytes 10682624 | tf_op jit(solution)/shard_map/while/body/eval_jaxpr/jhid,jhkd->jhik/dot_general | solution.py:36
  443.3 11.5 %fusion.64 = f32[128,4,64]{2,1,0:T(4,128)S(1)} fusion(f32[128,4,64,64]{2,3,1,0:T(8,128)} %get-tuple-element.362, f32[128,4,64]{2,1,0:T(4,128)S(1)} %max.11, f32[64]{0:T(128)} %dynamic_slice.33, f32[4,64,64]{1,2,0:T(8,128)S(1)} %dynamic-slice_convert_fusion.2), kind=kLoop, calls=%fused_computation.4.clone.1 | loop fusion | flops 8355840 | bytes 8716544 | tf_op jit(solution)/shard_map/while/body/eval_jaxpr/reduce_sum | solution.py:40
  455.1 12.5 %multiply_add_fusion.5 = f32[128,4,64,16]{2,3,1,0:T(8,128)} fusion(f32[128,4,64,16]{2,3,1,0:T(8,128)} %get-tuple-element.384, f32[128,4,64]{2,1,0:T(4,128)S(1)} %bitcast.105, f32[128,4,64,64]{2,3,1,0:T(8,128)} %get-tuple-element.362, f32[128,4,64]{2,1,0:T(4,128)S(1)} %max.11, f32[64]{0:T(128)} %dynamic_slice.33, ...), kind=kOutput, calls=%fused_computation.9.clone.1 | convolution fusion | flops 76546048 | bytes 13959424 | tf_op jit(solution)/shard_map/while/body/eval_jaxpr/jhik,jhkd->jhid/dot_general | solution.py:41
  472.8 25.2 %collective-permute-done = bf16[2,128,4,64,16]{1,4,3,2,0:T(8,128)(2,1)S(1)} collective-permute-done((bf16[2,128,4,64,16]{1,4,3,2,0:T(8,128)(2,1)}, bf16[2,128,4,64,16]{1,4,3,2,0:T(8,128)(2,1)S(1)}, u32[]{:S(2)}, u32[]{:S(2)}) %collective-permute-start) | collective-permute-done | bytes 2097184 | tf_op jit(solution)/shard_map/while/body/eval_jaxpr/ppermute | solution.py:77
  498.0 1.6 fusion.62
  499.6 5.4 copy.81
  505.0 3.3 copy.82
  508.3 11.7 %fusion.63 = (f32[128,4,64]{2,1,0:T(4,128)S(1)}, f32[128,4,64,64]{2,3,1,0:T(8,128)}) fusion(f32[64]{0:T(128)} %dynamic_slice.33, f32[4,64,64]{1,2,0:T(8,128)S(1)} %dynamic-slice_convert_fusion.2, bf16[128,4,64,16]{2,3,1,0:T(8,128)(2,1)} %copy-done.3, bf16[1,128,4,64,16]{3,4,2,1,0:T(8,128)(2,1)} %copy.81), kind=kOutput, calls=%fused_computation.2.clone.1 | convolution fusion | flops 73367552 | bytes 10682624 | tf_op jit(solution)/shard_map/while/body/eval_jaxpr/jhid,jhkd->jhik/dot_general | solution.py:36
  520.1 11.5 %fusion.64 = f32[128,4,64]{2,1,0:T(4,128)S(1)} fusion(f32[128,4,64,64]{2,3,1,0:T(8,128)} %get-tuple-element.362, f32[128,4,64]{2,1,0:T(4,128)S(1)} %max.11, f32[64]{0:T(128)} %dynamic_slice.33, f32[4,64,64]{1,2,0:T(8,128)S(1)} %dynamic-slice_convert_fusion.2), kind=kLoop, calls=%fused_computation.4.clone.1 | loop fusion | flops 8355840 | bytes 8716544 | tf_op jit(solution)/shard_map/while/body/eval_jaxpr/reduce_sum | solution.py:40
  531.9 12.5 %multiply_add_fusion.5 = f32[128,4,64,16]{2,3,1,0:T(8,128)} fusion(f32[128,4,64,16]{2,3,1,0:T(8,128)} %get-tuple-element.384, f32[128,4,64]{2,1,0:T(4,128)S(1)} %bitcast.105, f32[128,4,64,64]{2,3,1,0:T(8,128)} %get-tuple-element.362, f32[128,4,64]{2,1,0:T(4,128)S(1)} %max.11, f32[64]{0:T(128)} %dynamic_slice.33, ...), kind=kOutput, calls=%fused_computation.9.clone.1 | convolution fusion | flops 76546048 | bytes 13959424 | tf_op jit(solution)/shard_map/while/body/eval_jaxpr/jhik,jhkd->jhid/dot_general | solution.py:41
  549.6 25.2 %collective-permute-done = bf16[2,128,4,64,16]{1,4,3,2,0:T(8,128)(2,1)S(1)} collective-permute-done((bf16[2,128,4,64,16]{1,4,3,2,0:T(8,128)(2,1)}, bf16[2,128,4,64,16]{1,4,3,2,0:T(8,128)(2,1)S(1)}, u32[]{:S(2)}, u32[]{:S(2)}) %collective-permute-start) | collective-permute-done | bytes 2097184 | tf_op jit(solution)/shard_map/while/body/eval_jaxpr/ppermute | solution.py:77
  574.8 1.6 fusion.62
  576.4 5.4 copy.81
  581.8 3.3 copy.82
  585.1 11.7 %fusion.63 = (f32[128,4,64]{2,1,0:T(4,128)S(1)}, f32[128,4,64,64]{2,3,1,0:T(8,128)}) fusion(f32[64]{0:T(128)} %dynamic_slice.33, f32[4,64,64]{1,2,0:T(8,128)S(1)} %dynamic-slice_convert_fusion.2, bf16[128,4,64,16]{2,3,1,0:T(8,128)(2,1)} %copy-done.3, bf16[1,128,4,64,16]{3,4,2,1,0:T(8,128)(2,1)} %copy.81), kind=kOutput, calls=%fused_computation.2.clone.1 | convolution fusion | flops 73367552 | bytes 10682624 | tf_op jit(solution)/shard_map/while/body/eval_jaxpr/jhid,jhkd->jhik/dot_general | solution.py:36
  596.9 11.5 %fusion.64 = f32[128,4,64]{2,1,0:T(4,128)S(1)} fusion(f32[128,4,64,64]{2,3,1,0:T(8,128)} %get-tuple-element.362, f32[128,4,64]{2,1,0:T(4,128)S(1)} %max.11, f32[64]{0:T(128)} %dynamic_slice.33, f32[4,64,64]{1,2,0:T(8,128)S(1)} %dynamic-slice_convert_fusion.2), kind=kLoop, calls=%fused_computation.4.clone.1 | loop fusion | flops 8355840 | bytes 8716544 | tf_op jit(solution)/shard_map/while/body/eval_jaxpr/reduce_sum | solution.py:40
  608.7 12.5 %multiply_add_fusion.5 = f32[128,4,64,16]{2,3,1,0:T(8,128)} fusion(f32[128,4,64,16]{2,3,1,0:T(8,128)} %get-tuple-element.384, f32[128,4,64]{2,1,0:T(4,128)S(1)} %bitcast.105, f32[128,4,64,64]{2,3,1,0:T(8,128)} %get-tuple-element.362, f32[128,4,64]{2,1,0:T(4,128)S(1)} %max.11, f32[64]{0:T(128)} %dynamic_slice.33, ...), kind=kOutput, calls=%fused_computation.9.clone.1 | convolution fusion | flops 76546048 | bytes 13959424 | tf_op jit(solution)/shard_map/while/body/eval_jaxpr/jhik,jhkd->jhid/dot_general | solution.py:41
  623.8 6.4 %fusion.23 = bf16[128,4,64,16]{2,3,1,0:T(8,128)(2,1)} fusion(f32[128,4,64,16]{2,3,1,0:T(8,128)} %get-tuple-element.227, bf16[64,128,64,1]{2,0,3,1:T(8,128)(2,1)} %copy.69, bf16[64,4,16,1]{0,2,1,3:T(8,128)(2,1)} %bitcast.114, f32[128,4,64]{2,1,0:T(4,128)} %get-tuple-element.228), kind=kOutput, calls=%fused_computation.26 | convolution fusion | flops 70254592 | bytes 4333568 | tf_op jit(solution)/shard_map/ijc,chd->jhid/dot_general | solution.py:23
  630.2 4.5 copy.67
  (206 shorter events, 51.4 us)
Async XLA Ops:
  0.0 634.8 %copy-start = (bf16[64,64]{1,0:T(8,128)(2,1)S(1)}, bf16[64,64]{1,0:T(8,128)(2,1)}, u32[]{:S(2)}) copy-start(bf16[64,64]{1,0:T(8,128)(2,1)} %param.21) | copy-start | bytes 24580
  0.0 23.8 %copy-start.5 = (bf16[64,128,64]{1,2,0:T(8,128)(2,1)S(1)}, bf16[64,128,64]{1,2,0:T(8,128)(2,1)}, u32[]{:S(2)}) copy-start(bf16[64,128,64]{1,2,0:T(8,128)(2,1)} %param.12) | copy-start | bytes 3145732
  0.0 23.8 %copy-start.18 = (f32[64]{0:T(128)S(1)}, f32[64]{0:T(128)}, u32[]{:S(2)}) copy-start(f32[64]{0:T(128)} %param.14) | copy-start | bytes 772
  0.0 23.8 %copy-start.17 = (f32[64]{0:T(128)S(1)}, f32[64]{0:T(128)}, u32[]{:S(2)}) copy-start(f32[64]{0:T(128)} %param.15) | copy-start | bytes 772
  0.0 5.1 copy-start.19
  3.3 22.1 %copy-start.10 = (bf16[64,64]{1,0:T(8,128)(2,1)S(1)}, bf16[64,64]{1,0:T(8,128)(2,1)}, u32[]{:S(2)}) copy-start(bf16[64,64]{1,0:T(8,128)(2,1)} %param.17) | copy-start | bytes 24580
  3.3 22.2 %copy-start.11 = (bf16[64,64]{1,0:T(8,128)(2,1)S(1)}, bf16[64,64]{1,0:T(8,128)(2,1)}, u32[]{:S(2)}) copy-start(bf16[64,64]{1,0:T(8,128)(2,1)} %param.18) | copy-start | bytes 24580
  19.3 29.1 %all-to-all-start = ((bf16[8,2,8192]{2,1,0:T(2,128)(2,1)}), bf16[8,2,8192]{2,1,0:T(2,128)(2,1)S(1)}, u32[]{:S(2)}, u32[]{:S(2)}) async-start(bf16[8,2,8192]{2,1,0:T(2,128)(2,1)} %reshape.49), calls=%async_computation | async-start | bytes 524288 | tf_op jit(solution)/shard_map/all_to_all | solution.py:30
  25.4 3.6 copy-start.12
  33.8 13.8 %copy-start.13 = (bf16[64,64]{1,0:T(8,128)(2,1)S(1)}, bf16[64,64]{1,0:T(8,128)(2,1)}, u32[]{:S(2)}) copy-start(bf16[64,64]{1,0:T(8,128)(2,1)} %param.20) | copy-start | bytes 24580
  33.8 14.5 %copy-start.14 = (s32[512]{0:T(512)S(1)}, s32[512]{0:T(512)}, u32[]{:S(2)}) copy-start(s32[512]{0:T(512)} %param.13) | copy-start | bytes 6148
  87.3 1.9 copy-start.15
  87.3 26.7 %collective-permute-start = (bf16[2,128,4,64,16]{1,4,3,2,0:T(8,128)(2,1)}, bf16[2,128,4,64,16]{1,4,3,2,0:T(8,128)(2,1)S(1)}, u32[]{:S(2)}, u32[]{:S(2)}) collective-permute-start(bf16[2,128,4,64,16]{1,4,3,2,0:T(8,128)(2,1)} %get-tuple-element.385), channel_id=1, source_target_pairs={{0,1},{1,2},{2,3},{3,4},{4,5},{5,6},{6,7},{7,0},{8,9},{9,10},{10,1... | collective-permute-start | bytes 6291464 | tf_op jit(solution)/shard_map/while/body/eval_jaxpr/ppermute | solution.py:77
  114.0 7.0 %copy-start.1 = (bf16[2,128,4,64,16]{1,4,3,2,0:T(8,128)(2,1)}, bf16[2,128,4,64,16]{1,4,3,2,0:T(8,128)(2,1)S(1)}, u32[]{:S(2)}) copy-start(bf16[2,128,4,64,16]{1,4,3,2,0:T(8,128)(2,1)S(1)} %collective-permute-done) | copy-start | bytes 6291460 | tf_op jit(solution)/shard_map/while
  136.0 11.6 %copy-start.7 = (f32[128,4,64]{2,1,0:T(4,128)S(1)}, f32[128,4,64]{2,1,0:T(4,128)}, u32[]{:S(2)}) copy-start(f32[128,4,64]{2,1,0:T(4,128)} %get-tuple-element.383) | copy-start | bytes 393220 | tf_op jit(solution)/shard_map/while
  147.8 12.6 %copy-start.8 = (f32[64,8,64]{2,1,0:T(8,128)}, f32[64,8,64]{2,1,0:T(8,128)S(1)}, u32[]{:S(2)}) copy-start(f32[64,8,64]{2,1,0:T(8,128)S(1)} %get-tuple-element.363) | copy-start | bytes 393220 | tf_op jit(solution)/shard_map/while
  147.8 12.6 %copy-start.2 = (bf16[2,128,4,64,16]{1,4,3,2,0:T(8,128)(2,1)S(1)}, bf16[2,128,4,64,16]{1,4,3,2,0:T(8,128)(2,1)}, u32[]{:S(2)}) copy-start(bf16[2,128,4,64,16]{1,4,3,2,0:T(8,128)(2,1)} %copy-done.1) | copy-start | bytes 6291460 | tf_op jit(solution)/shard_map/while
  160.4 2.3 copy-start.4
  160.4 2.3 copy-start.16
  164.1 1.4 copy-start.15
  164.1 26.7 %collective-permute-start = (bf16[2,128,4,64,16]{1,4,3,2,0:T(8,128)(2,1)}, bf16[2,128,4,64,16]{1,4,3,2,0:T(8,128)(2,1)S(1)}, u32[]{:S(2)}, u32[]{:S(2)}) collective-permute-start(bf16[2,128,4,64,16]{1,4,3,2,0:T(8,128)(2,1)} %get-tuple-element.385), channel_id=1, source_target_pairs={{0,1},{1,2},{2,3},{3,4},{4,5},{5,6},{6,7},{7,0},{8,9},{9,10},{10,1... | collective-permute-start | bytes 6291464 | tf_op jit(solution)/shard_map/while/body/eval_jaxpr/ppermute | solution.py:77
  190.8 7.0 %copy-start.1 = (bf16[2,128,4,64,16]{1,4,3,2,0:T(8,128)(2,1)}, bf16[2,128,4,64,16]{1,4,3,2,0:T(8,128)(2,1)S(1)}, u32[]{:S(2)}) copy-start(bf16[2,128,4,64,16]{1,4,3,2,0:T(8,128)(2,1)S(1)} %collective-permute-done) | copy-start | bytes 6291460 | tf_op jit(solution)/shard_map/while
  212.8 11.6 %copy-start.7 = (f32[128,4,64]{2,1,0:T(4,128)S(1)}, f32[128,4,64]{2,1,0:T(4,128)}, u32[]{:S(2)}) copy-start(f32[128,4,64]{2,1,0:T(4,128)} %get-tuple-element.383) | copy-start | bytes 393220 | tf_op jit(solution)/shard_map/while
  224.6 12.6 %copy-start.8 = (f32[64,8,64]{2,1,0:T(8,128)}, f32[64,8,64]{2,1,0:T(8,128)S(1)}, u32[]{:S(2)}) copy-start(f32[64,8,64]{2,1,0:T(8,128)S(1)} %get-tuple-element.363) | copy-start | bytes 393220 | tf_op jit(solution)/shard_map/while
  224.6 12.6 %copy-start.2 = (bf16[2,128,4,64,16]{1,4,3,2,0:T(8,128)(2,1)S(1)}, bf16[2,128,4,64,16]{1,4,3,2,0:T(8,128)(2,1)}, u32[]{:S(2)}) copy-start(bf16[2,128,4,64,16]{1,4,3,2,0:T(8,128)(2,1)} %copy-done.1) | copy-start | bytes 6291460 | tf_op jit(solution)/shard_map/while
  237.2 2.3 copy-start.4
  237.2 2.3 copy-start.16
  240.9 26.7 %collective-permute-start = (bf16[2,128,4,64,16]{1,4,3,2,0:T(8,128)(2,1)}, bf16[2,128,4,64,16]{1,4,3,2,0:T(8,128)(2,1)S(1)}, u32[]{:S(2)}, u32[]{:S(2)}) collective-permute-start(bf16[2,128,4,64,16]{1,4,3,2,0:T(8,128)(2,1)} %get-tuple-element.385), channel_id=1, source_target_pairs={{0,1},{1,2},{2,3},{3,4},{4,5},{5,6},{6,7},{7,0},{8,9},{9,10},{10,1... | collective-permute-start | bytes 6291464 | tf_op jit(solution)/shard_map/while/body/eval_jaxpr/ppermute | solution.py:77
  267.6 7.0 %copy-start.1 = (bf16[2,128,4,64,16]{1,4,3,2,0:T(8,128)(2,1)}, bf16[2,128,4,64,16]{1,4,3,2,0:T(8,128)(2,1)S(1)}, u32[]{:S(2)}) copy-start(bf16[2,128,4,64,16]{1,4,3,2,0:T(8,128)(2,1)S(1)} %collective-permute-done) | copy-start | bytes 6291460 | tf_op jit(solution)/shard_map/while
  289.6 11.6 %copy-start.7 = (f32[128,4,64]{2,1,0:T(4,128)S(1)}, f32[128,4,64]{2,1,0:T(4,128)}, u32[]{:S(2)}) copy-start(f32[128,4,64]{2,1,0:T(4,128)} %get-tuple-element.383) | copy-start | bytes 393220 | tf_op jit(solution)/shard_map/while
  301.4 12.6 %copy-start.8 = (f32[64,8,64]{2,1,0:T(8,128)}, f32[64,8,64]{2,1,0:T(8,128)S(1)}, u32[]{:S(2)}) copy-start(f32[64,8,64]{2,1,0:T(8,128)S(1)} %get-tuple-element.363) | copy-start | bytes 393220 | tf_op jit(solution)/shard_map/while
  301.4 12.6 %copy-start.2 = (bf16[2,128,4,64,16]{1,4,3,2,0:T(8,128)(2,1)S(1)}, bf16[2,128,4,64,16]{1,4,3,2,0:T(8,128)(2,1)}, u32[]{:S(2)}) copy-start(bf16[2,128,4,64,16]{1,4,3,2,0:T(8,128)(2,1)} %copy-done.1) | copy-start | bytes 6291460 | tf_op jit(solution)/shard_map/while
  314.0 2.3 copy-start.4
  314.0 2.3 copy-start.16
  317.7 1.4 copy-start.15
  317.7 26.7 %collective-permute-start = (bf16[2,128,4,64,16]{1,4,3,2,0:T(8,128)(2,1)}, bf16[2,128,4,64,16]{1,4,3,2,0:T(8,128)(2,1)S(1)}, u32[]{:S(2)}, u32[]{:S(2)}) collective-permute-start(bf16[2,128,4,64,16]{1,4,3,2,0:T(8,128)(2,1)} %get-tuple-element.385), channel_id=1, source_target_pairs={{0,1},{1,2},{2,3},{3,4},{4,5},{5,6},{6,7},{7,0},{8,9},{9,10},{10,1... | collective-permute-start | bytes 6291464 | tf_op jit(solution)/shard_map/while/body/eval_jaxpr/ppermute | solution.py:77
  344.4 7.0 %copy-start.1 = (bf16[2,128,4,64,16]{1,4,3,2,0:T(8,128)(2,1)}, bf16[2,128,4,64,16]{1,4,3,2,0:T(8,128)(2,1)S(1)}, u32[]{:S(2)}) copy-start(bf16[2,128,4,64,16]{1,4,3,2,0:T(8,128)(2,1)S(1)} %collective-permute-done) | copy-start | bytes 6291460 | tf_op jit(solution)/shard_map/while
  366.4 11.6 %copy-start.7 = (f32[128,4,64]{2,1,0:T(4,128)S(1)}, f32[128,4,64]{2,1,0:T(4,128)}, u32[]{:S(2)}) copy-start(f32[128,4,64]{2,1,0:T(4,128)} %get-tuple-element.383) | copy-start | bytes 393220 | tf_op jit(solution)/shard_map/while
  378.2 12.6 %copy-start.8 = (f32[64,8,64]{2,1,0:T(8,128)}, f32[64,8,64]{2,1,0:T(8,128)S(1)}, u32[]{:S(2)}) copy-start(f32[64,8,64]{2,1,0:T(8,128)S(1)} %get-tuple-element.363) | copy-start | bytes 393220 | tf_op jit(solution)/shard_map/while
  378.2 12.6 %copy-start.2 = (bf16[2,128,4,64,16]{1,4,3,2,0:T(8,128)(2,1)S(1)}, bf16[2,128,4,64,16]{1,4,3,2,0:T(8,128)(2,1)}, u32[]{:S(2)}) copy-start(bf16[2,128,4,64,16]{1,4,3,2,0:T(8,128)(2,1)} %copy-done.1) | copy-start | bytes 6291460 | tf_op jit(solution)/shard_map/while
  390.8 2.3 copy-start.4
  390.8 2.3 copy-start.16
  394.5 26.7 %collective-permute-start = (bf16[2,128,4,64,16]{1,4,3,2,0:T(8,128)(2,1)}, bf16[2,128,4,64,16]{1,4,3,2,0:T(8,128)(2,1)S(1)}, u32[]{:S(2)}, u32[]{:S(2)}) collective-permute-start(bf16[2,128,4,64,16]{1,4,3,2,0:T(8,128)(2,1)} %get-tuple-element.385), channel_id=1, source_target_pairs={{0,1},{1,2},{2,3},{3,4},{4,5},{5,6},{6,7},{7,0},{8,9},{9,10},{10,1... | collective-permute-start | bytes 6291464 | tf_op jit(solution)/shard_map/while/body/eval_jaxpr/ppermute | solution.py:77
  421.2 7.0 %copy-start.1 = (bf16[2,128,4,64,16]{1,4,3,2,0:T(8,128)(2,1)}, bf16[2,128,4,64,16]{1,4,3,2,0:T(8,128)(2,1)S(1)}, u32[]{:S(2)}) copy-start(bf16[2,128,4,64,16]{1,4,3,2,0:T(8,128)(2,1)S(1)} %collective-permute-done) | copy-start | bytes 6291460 | tf_op jit(solution)/shard_map/while
  443.2 11.6 %copy-start.7 = (f32[128,4,64]{2,1,0:T(4,128)S(1)}, f32[128,4,64]{2,1,0:T(4,128)}, u32[]{:S(2)}) copy-start(f32[128,4,64]{2,1,0:T(4,128)} %get-tuple-element.383) | copy-start | bytes 393220 | tf_op jit(solution)/shard_map/while
  455.0 12.6 %copy-start.8 = (f32[64,8,64]{2,1,0:T(8,128)}, f32[64,8,64]{2,1,0:T(8,128)S(1)}, u32[]{:S(2)}) copy-start(f32[64,8,64]{2,1,0:T(8,128)S(1)} %get-tuple-element.363) | copy-start | bytes 393220 | tf_op jit(solution)/shard_map/while
  455.1 12.6 %copy-start.2 = (bf16[2,128,4,64,16]{1,4,3,2,0:T(8,128)(2,1)S(1)}, bf16[2,128,4,64,16]{1,4,3,2,0:T(8,128)(2,1)}, u32[]{:S(2)}) copy-start(bf16[2,128,4,64,16]{1,4,3,2,0:T(8,128)(2,1)} %copy-done.1) | copy-start | bytes 6291460 | tf_op jit(solution)/shard_map/while
  467.6 2.3 copy-start.4
  467.6 2.3 copy-start.16
  471.3 26.7 %collective-permute-start = (bf16[2,128,4,64,16]{1,4,3,2,0:T(8,128)(2,1)}, bf16[2,128,4,64,16]{1,4,3,2,0:T(8,128)(2,1)S(1)}, u32[]{:S(2)}, u32[]{:S(2)}) collective-permute-start(bf16[2,128,4,64,16]{1,4,3,2,0:T(8,128)(2,1)} %get-tuple-element.385), channel_id=1, source_target_pairs={{0,1},{1,2},{2,3},{3,4},{4,5},{5,6},{6,7},{7,0},{8,9},{9,10},{10,1... | collective-permute-start | bytes 6291464 | tf_op jit(solution)/shard_map/while/body/eval_jaxpr/ppermute | solution.py:77
  498.0 7.0 %copy-start.1 = (bf16[2,128,4,64,16]{1,4,3,2,0:T(8,128)(2,1)}, bf16[2,128,4,64,16]{1,4,3,2,0:T(8,128)(2,1)S(1)}, u32[]{:S(2)}) copy-start(bf16[2,128,4,64,16]{1,4,3,2,0:T(8,128)(2,1)S(1)} %collective-permute-done) | copy-start | bytes 6291460 | tf_op jit(solution)/shard_map/while
  520.1 11.6 %copy-start.7 = (f32[128,4,64]{2,1,0:T(4,128)S(1)}, f32[128,4,64]{2,1,0:T(4,128)}, u32[]{:S(2)}) copy-start(f32[128,4,64]{2,1,0:T(4,128)} %get-tuple-element.383) | copy-start | bytes 393220 | tf_op jit(solution)/shard_map/while
  531.8 12.6 %copy-start.8 = (f32[64,8,64]{2,1,0:T(8,128)}, f32[64,8,64]{2,1,0:T(8,128)S(1)}, u32[]{:S(2)}) copy-start(f32[64,8,64]{2,1,0:T(8,128)S(1)} %get-tuple-element.363) | copy-start | bytes 393220 | tf_op jit(solution)/shard_map/while
  531.9 12.6 %copy-start.2 = (bf16[2,128,4,64,16]{1,4,3,2,0:T(8,128)(2,1)S(1)}, bf16[2,128,4,64,16]{1,4,3,2,0:T(8,128)(2,1)}, u32[]{:S(2)}) copy-start(bf16[2,128,4,64,16]{1,4,3,2,0:T(8,128)(2,1)} %copy-done.1) | copy-start | bytes 6291460 | tf_op jit(solution)/shard_map/while
  544.4 2.3 copy-start.4
  544.4 2.3 copy-start.16
  548.1 26.7 %collective-permute-start = (bf16[2,128,4,64,16]{1,4,3,2,0:T(8,128)(2,1)}, bf16[2,128,4,64,16]{1,4,3,2,0:T(8,128)(2,1)S(1)}, u32[]{:S(2)}, u32[]{:S(2)}) collective-permute-start(bf16[2,128,4,64,16]{1,4,3,2,0:T(8,128)(2,1)} %get-tuple-element.385), channel_id=1, source_target_pairs={{0,1},{1,2},{2,3},{3,4},{4,5},{5,6},{6,7},{7,0},{8,9},{9,10},{10,1... | collective-permute-start | bytes 6291464 | tf_op jit(solution)/shard_map/while/body/eval_jaxpr/ppermute | solution.py:77
  574.8 7.0 %copy-start.1 = (bf16[2,128,4,64,16]{1,4,3,2,0:T(8,128)(2,1)}, bf16[2,128,4,64,16]{1,4,3,2,0:T(8,128)(2,1)S(1)}, u32[]{:S(2)}) copy-start(bf16[2,128,4,64,16]{1,4,3,2,0:T(8,128)(2,1)S(1)} %collective-permute-done) | copy-start | bytes 6291460 | tf_op jit(solution)/shard_map/while
  596.9 11.6 %copy-start.7 = (f32[128,4,64]{2,1,0:T(4,128)S(1)}, f32[128,4,64]{2,1,0:T(4,128)}, u32[]{:S(2)}) copy-start(f32[128,4,64]{2,1,0:T(4,128)} %get-tuple-element.383) | copy-start | bytes 393220 | tf_op jit(solution)/shard_map/while
  608.6 12.6 %copy-start.8 = (f32[64,8,64]{2,1,0:T(8,128)}, f32[64,8,64]{2,1,0:T(8,128)S(1)}, u32[]{:S(2)}) copy-start(f32[64,8,64]{2,1,0:T(8,128)S(1)} %get-tuple-element.363) | copy-start | bytes 393220 | tf_op jit(solution)/shard_map/while
  608.7 12.6 %copy-start.2 = (bf16[2,128,4,64,16]{1,4,3,2,0:T(8,128)(2,1)S(1)}, bf16[2,128,4,64,16]{1,4,3,2,0:T(8,128)(2,1)}, u32[]{:S(2)}) copy-start(bf16[2,128,4,64,16]{1,4,3,2,0:T(8,128)(2,1)} %copy-done.1) | copy-start | bytes 6291460 | tf_op jit(solution)/shard_map/while
  621.2 2.3 copy-start.4
  621.2 2.3 copy-start.16
  623.8 11.0 %copy-start.6 = (bf16[64,128,64]{1,2,0:T(8,128)(2,1)S(1)}, bf16[64,128,64]{1,2,0:T(8,128)(2,1)}, u32[]{:S(2)}) copy-start(bf16[64,128,64]{1,2,0:T(8,128)(2,1)} %param.12) | copy-start | bytes 3145732
  (12 other events, 16.7 us)
where the time goes:
time: 645 us; the launch traced here: 637 us
  matrix products  202 us (31%)
  waiting for transfers between devices  176 us (27%)
  local copies, waits for them, and re-layouts  131 us (20%)
  other arithmetic  108 us (17%)
  blocking collectives  12.4 us (2%)
    ppermute x7, waiting for transfers between devices, shift_step(): kv_blk = lax.ppermute(kv_blk, 'row', next_hop)  176 us
    dot_general x8, matrix products, attend_block(): jnp.einsum('jhik,jhkd->jhid', p_exp.astype(jnp.bfloat16), kv_blk[1], pref...  99.5 us
    dot_general x8, matrix products, attend_block(): jnp.einsum('jhid,jhkd->jhik', query, kv_blk[0], preferred_element_type=jn...  93.1 us
    reduce_sum x8, other arithmetic, attend_block(): run_sum = run_sum * rescale + jnp.sum(p_exp, axis=-1)  92.2 us
    while x140, local copies, waits for them, and re-layouts  86.6 us
  transfers between devices with their start and end apart: 8, of which 7 were waited for; matrix products, arithmetic and copies ran while one was open for 5% of the time, Pallas kernels for 0%

commit v1 on v0

v1 whole, which is shorter than its diff:
```python
import functools
import math

import jax
import jax.numpy as jnp
from jax import lax
from jax.experimental import pallas as pl
from jax.experimental.pallas import tpu as pltpu
from jax.sharding import PartitionSpec as P

LN_EPS = 1e-5
MASK_FILL = -1e9
MESH = pl.DeviceIdType.MESH
F32, BF16 = jnp.float32, jnp.bfloat16
NT = (((1,), (1,)), ((), ()))
PAD = 8


def mm(a, b):
    return jnp.dot(a, b, preferred_element_type=F32)


def mm_nt(a, b):
    return lax.dot_general(a, b, NT, preferred_element_type=F32)


def tr(w):
    return jnp.transpose(w.astype(F32)).astype(BF16)


def block_diag2(w):
    z = jnp.zeros_like(w)
    return jnp.concatenate([jnp.concatenate([w, z], 1), jnp.concatenate([z, w], 1)], 0)


def remote(src, dst, send, recv, dev):
    return pltpu.make_async_remote_copy(src_ref=src, dst_ref=dst, send_sem=send, recv_sem=recv, device_id=dev, device_id_type=MESH)


def gather_kernel(rows, cols, z_ref, gamma_ref, beta_ref, wb_ref, a_ref, bias_ref, stage, bsc, send, a_sem, x_sem, y_sem, f_sem):
    ti, ch, tj = z_ref.shape
    heads = wb_ref.shape[0]
    cj = tj // rows
    hj = cj // 2
    pitch = rows * hj + PAD
    me_r, me_c = lax.axis_index('row'), lax.axis_index('col')
    core = me_r % 2
    partner = me_r + 1 - 2 * core

    barrier = pltpu.get_barrier_semaphore()
    for d in range(1, rows):
        pl.semaphore_signal(barrier, inc=1, device_id={'row': (me_r + d) % rows}, device_id_type=MESH)
    for d in range(1, cols):
        pl.semaphore_signal(barrier, inc=1, device_id={'col': (me_c + d) % cols}, device_id_type=MESH)

    gam = jnp.transpose(jnp.broadcast_to(gamma_ref[...], (tj, ch)))
    bet = jnp.transpose(jnp.broadcast_to(beta_ref[...], (tj, ch)))
    group = 4
    wb = wb_ref[...].astype(F32)
    wb16 = jnp.concatenate([wb] * group, 0)
    wb16 = jnp.concatenate([wb16] * group, 1)
    r_id = lax.broadcasted_iota(jnp.int32, wb16.shape, 0) // heads
    c_id = lax.broadcasted_iota(jnp.int32, wb16.shape, 1) // ch
    wb16 = jnp.where(r_id == c_id, wb16, 0.0).astype(BF16)

    def norm_step(t, _):
        x = z_ref[pl.ds(t * group, group)].astype(F32)
        mean = jnp.sum(x, axis=1, keepdims=True) * (1.0 / ch)
        cen = x - mean
        var = jnp.sum(cen * cen, axis=1, keepdims=True) * (1.0 / ch)
        n = cen * lax.rsqrt(var + LN_EPS) * gam + bet
        nb = n.astype(BF16)
        bsc[pl.ds(pl.multiple_of(t * group * heads, group * heads), group * heads), :] = mm(wb16, nb.reshape(group * ch, tj))
        for q in range(group):
            t4 = jnp.transpose(n[q]).reshape(rows, 2, hj, ch)
            packed = jnp.concatenate([t4[:, 0], t4[:, 1]], axis=-1).reshape(rows * hj, 2 * ch)
            stage[pl.ds(pl.multiple_of((t * group + q) * pitch, 8), rows * hj), :] = packed
        return 0

    lax.fori_loop(0, ti // group, norm_step, 0)

    my_rows = pl.ds(pl.multiple_of(me_r * ti, ti), ti)
    for h in range(heads):
        bias_ref[me_c, h, my_rows, :] = bsc[pl.ds(h, ti, stride=heads), :].astype(BF16)

    pl.semaphore_wait(barrier, rows + cols - 2)

    def x_copy(d, src_row):
        rs = pl.ds(pl.multiple_of(src_row * ti, ti), ti)
        return remote(bias_ref.at[me_c, :, rs, :], bias_ref.at[me_c, :, rs, :], x_sem.at[0, d], x_sem.at[1, d], {'row': (me_r + d) % rows})

    def a_copy(d, dst_row, src_row):
        rs = pl.ds(pl.multiple_of(src_row * ti, ti), ti)
        return remote(send.at[dst_row], a_ref.at[:, rs, :], a_sem.at[0, d], a_sem.at[1, d], {'row': (me_r + d) % rows})

    def piece(dst_row, jp):
        return stage[pl.ds(dst_row * hj + jp, ti, stride=pitch), :].astype(BF16)

    order = [4, 3, 5, 2, 6, 1, 7] if rows == 8 else list(range(1, rows))
    for d in order:
        x_copy(d, me_r).start()
    last = None
    for d in order:
        dst = (me_r + d) % rows
        for jp in range(hj):
            send[dst, jp] = piece(dst, jp)
        if last is not None:
            last.start()
        last = a_copy(d, dst, me_r)
    for jp in range(hj):
        a_ref[jp, my_rows, :] = piece(me_r, jp)
    last.start()

    hh = heads // 2
    mine, other = pl.ds(core * hh, hh), pl.ds((1 - core) * hh, hh)

    def y_copy(d, blk):
        return remote(bias_ref.at[blk, mine], bias_ref.at[blk, mine], y_sem.at[0, d], y_sem.at[1, d], {'col': (me_c + d) % cols})

    def f_copy(d, blk, part):
        return remote(bias_ref.at[blk, part], bias_ref.at[blk, part], f_sem.at[0, d], f_sem.at[1, d], {'row': partner})

    for d in order:
        x_copy(d, (me_r + rows - d) % rows).wait_recv()
    y_order = [2, 1, 3] if cols == 4 else list(range(1, cols))
    for d in y_order:
        y_copy(d, me_c).start()
    for d in y_order:
        blk = (me_c + cols - d) % cols
        y_copy(d, blk).wait_recv()
        f_copy(d, blk, mine).start()
    for d in y_order:
        f_copy(d, (me_c + cols - d) % cols, other).wait_recv()
    for d in order:
        a_copy(d, me_r, (me_r + rows - d) % rows).wait_recv()
    for d in order:
        x_copy(d, me_r).wait_send()
        a_copy(d, (me_r + d) % rows, me_r).wait_send()
    for d in y_order:
        y_copy(d, me_c).wait_send()
        f_copy(d, me_c, mine).wait_send()


def attend_kernel(a_ref, bias_ref, mask_ref, wq_ref, wk_ref, wv_ref, wg_ref, out_ref, qt, vt, gt, kk, bf, ga):
    hj, n, two_ch = a_ref.shape
    cols, heads, _, tj = bias_ref.shape
    ch = two_ch // 2
    e = wq_ref.shape[1] // heads
    proj = heads * e

    w3 = jnp.concatenate([tr(wq_ref[...]), tr(wv_ref[...]), tr(wg_ref[...])], 0)
    w6 = block_diag2(w3)
    wk2 = block_diag2(wk_ref[...])
    q_scale = 1.0 / math.sqrt(e)

    fill = jnp.where(mask_ref[...] > 0, 0.0, MASK_FILL).astype(F32)
    fill_col = jnp.transpose(jnp.broadcast_to(fill, (tj, n)))

    def bias_step(t, _):
        bf[t] = bias_ref[t // heads, t % heads].astype(F32) + fill_col
        return 0

    lax.fori_loop(0, cols * heads, bias_step, 0)

    def proj_step(jp, _):
        a = a_ref[jp]
        r = mm_nt(w6, a)
        for half in range(2):
            o = half * 3 * proj
            dst = pl.ds(half * proj, proj)
            q = (r[o:o + proj] * q_scale).astype(BF16)
            g = jax.nn.sigmoid(r[o + 2 * proj:o + 3 * proj])
            vt[jp, dst, :] = r[o + proj:o + 2 * proj].astype(BF16)
            for ib in range(cols):
                qt[jp, ib, dst, :] = q[:, ib * tj:(ib + 1) * tj]
                gt[jp, ib, dst, :] = g[:, ib * tj:(ib + 1) * tj]
        kk[jp] = mm(a, wk2).astype(BF16)
        return 0

    lax.fori_loop(0, hj, proj_step, 0)

    def unit(t, _):
        ib, jp = t // hj, t % hj
        for h in range(heads):
            z16 = jnp.zeros((e, tj), BF16)
            rhs = []
            for half in range(2):
                for hh in range(heads):
                    if hh == h:
                        qv = qt[jp, ib, half * proj + h * e:half * proj + (h + 1) * e, :]
                        pair = [qv, z16] if half == 0 else [z16, qv]
                        rhs.append(jnp.concatenate(pair, 1))
                    else:
                        rhs.append(jnp.zeros((e, 2 * tj), BF16))
            rhs = jnp.concatenate(rhs, 0)
            bb = bf[ib * heads + h]
            s = mm(kk[jp], rhs) + jnp.concatenate([bb, bb], 1)
            m = jnp.max(s, axis=0, keepdims=True)
            p = jnp.exp(s - m)
            l = jnp.sum(p, axis=0, keepdims=True)
            v2 = jnp.concatenate([vt[jp, h * e:(h + 1) * e, :], vt[jp, proj + h * e:proj + (h + 1) * e, :]], 0)
            o = mm(v2, p.astype(BF16))
            for half in range(2):
                lanes = slice(half * tj, (half + 1) * tj)
                rs = slice(half * proj + h * e, half * proj + (h + 1) * e)
                ga[rs, :] = gt[jp, ib, rs, :] * (o[half * e:(half + 1) * e, lanes] / l[:, lanes])
        out_ref[jp, pl.ds(pl.multiple_of(ib * tj, tj), tj), :] = jnp.transpose(ga[...]).astype(BF16)
        return 0

    lax.fori_loop(0, cols * hj, unit, 0)


def return_kernel(rows, g_ref, out_ref, sem):
    hj, n, lanes = g_ref.shape
    ti = n // rows
    me_r = lax.axis_index('row')
    barrier = pltpu.get_barrier_semaphore()
    for d in range(1, rows):
        pl.semaphore_signal(barrier, inc=1, device_id={'row': (me_r + d) % rows}, device_id_type=MESH)
    pl.semaphore_wait(barrier, rows - 1)

    def copy(d, dst_row, slot):
        rs = pl.ds(pl.multiple_of(dst_row * ti, ti), ti)
        return remote(g_ref.at[:, rs, :], out_ref.at[slot], sem.at[0, d], sem.at[1, d], {'row': (me_r + d) % rows})

    order = [4, 3, 5, 2, 6, 1, 7] if rows == 8 else list(range(1, rows))
    for d in order:
        copy(d, (me_r + d) % rows, me_r).start()
    out_ref[me_r] = g_ref[:, pl.ds(pl.multiple_of(me_r * ti, ti), ti), :]
    for d in order:
        copy(d, me_r, (me_r + rows - d) % rows).wait_recv()
    for d in order:
        copy(d, (me_r + d) % rows, me_r).wait_send()


def finish_kernel(g_ref, z_ref, wo_ref, out_ref, stage):
    rows, hj, ti, lanes = g_ref.shape
    ch, tj = z_ref.shape[1:]
    pitch = ti + PAD
    n_rj = rows * hj
    wo = tr(wo_ref[...])
    wo = jnp.concatenate([wo, jnp.zeros_like(wo)], 1)

    def widen(t, _):
        for jp in range(hj):
            stage[pl.ds(pl.multiple_of((t * hj + jp) * pitch, 8), ti), :] = g_ref[t, jp].astype(F32)
        return 0

    lax.fori_loop(0, rows, widen, 0)

    group = 4

    def step(t, _):
        for q in range(group):
            i = t * group + q
            x = stage[pl.ds(i, n_rj, stride=pitch), :]
            y = pltpu.roll(x, ch, 1)
            x2 = jnp.concatenate([x.reshape(rows, 1, hj, lanes), y.reshape(rows, 1, hj, lanes)], 1).reshape(tj, lanes).astype(BF16)
            out_ref[i] = (mm_nt(wo, x2) + z_ref[i].astype(F32)).astype(BF16)
        return 0

    lax.fori_loop(0, ti // group, step, 0)


VM = pl.BlockSpec(memory_space=pltpu.VMEM)


def solution(mesh):
    rows, cols = mesh.shape['row'], mesh.shape['col']

    def body(pair_tile, res_mask, ln_gamma, ln_beta, w_q, w_k, w_v, w_b, w_g, w_o):
        ti, tj, ch = pair_tile.shape
        heads = w_b.shape[1]
        proj = w_q.shape[1]
        n = ti * rows
        hj = tj // rows // 2
        z = jnp.transpose(pair_tile, (0, 2, 1))
        dma = pltpu.SemaphoreType.DMA
        a_cols, bias = pl.pallas_call(
            functools.partial(gather_kernel, rows, cols),
            out_shape=(jax.ShapeDtypeStruct((hj, n, 2 * ch), BF16), jax.ShapeDtypeStruct((cols, heads, n, tj), BF16)),
            in_specs=[VM] * 4,
            out_specs=(VM, VM),
            scratch_shapes=[
                pltpu.VMEM((ti * (rows * hj + PAD), 2 * ch), F32),
                pltpu.VMEM((ti * heads, tj), F32),
                pltpu.VMEM((rows, hj, ti, 2 * ch), BF16),
                dma((2, rows)), dma((2, rows)), dma((2, cols)), dma((2, cols)),
            ],
            compiler_params=pltpu.CompilerParams(collective_id=0, has_side_effects=True),
            name='gather',
        )(z, ln_gamma.reshape(1, ch), ln_beta.reshape(1, ch), w_b.T)
        gated = pl.pallas_call(
            attend_kernel,
            out_shape=jax.ShapeDtypeStruct((hj, n, 2 * ch), BF16),
            in_specs=[VM] * 7,
            out_specs=VM,
            scratch_shapes=[
                pltpu.VMEM((hj, cols, 2 * proj, tj), BF16),
                pltpu.VMEM((hj, 2 * proj, n), BF16),
                pltpu.VMEM((hj, cols, 2 * proj, tj), F32),
                pltpu.VMEM((hj, n, 2 * proj), BF16),
                pltpu.VMEM((cols * heads, n, tj), F32),
                pltpu.VMEM((2 * proj, tj), F32),
            ],
            name='attend',
        )(a_cols, bias, res_mask.reshape(1, n), w_q, w_k, w_v, w_g)
        back = pl.pallas_call(
            functools.partial(return_kernel, rows),
            out_shape=jax.ShapeDtypeStruct((rows, hj, ti, 2 * ch), BF16),
            in_specs=[VM],
            out_specs=VM,
            scratch_shapes=[dma((2, rows))],
            compiler_params=pltpu.CompilerParams(collective_id=1, has_side_effects=True),
            name='back',
        )(gated)
        out = pl.pallas_call(
            finish_kernel,
            out_shape=jax.ShapeDtypeStruct((ti, ch, tj), BF16),
            in_specs=[VM] * 3,
            out_specs=VM,
            scratch_shapes=[pltpu.VMEM((rows * hj * (ti + PAD), 2 * ch), F32)],
            name='finish',
        )(back, z, w_o)
        return jnp.transpose(out, (0, 2, 1))

    tile_spec = P(('data', 'row'), 'col', None)
    return jax.shard_map(body, mesh=mesh, in_specs=(tile_spec, P('data'), P(), P(), P(), P(), P(), P(), P(), P()), out_specs=tile_spec, check_vma=False)
```

time: 645 us -> 122 us (0.19)
  the two profiles are of different devices: /device:TPU:96 before, /device:TPU:97 now
where the time goes in v1:
time: 122 us
  Pallas kernels  122 us (100%)
    pallas_call x1, Pallas kernels, body(): pl.pallas_call(attend_kernel, out_shape=jax.ShapeDtypeStruct((hj, n, 2 *...  61.2 us
    pallas_call x1, Pallas kernels, body(): pl.pallas_call(functools.partial(gather_kernel, rows, cols), out_shape=(j...  36.4 us
    pallas_call x1, Pallas kernels, body(): pl.pallas_call(functools.partial(return_kernel, rows), out_shape=jax.Shap...  17.4 us
    pallas_call x1, Pallas kernels, body(): pl.pallas_call(finish_kernel, out_shape=jax.ShapeDtypeStruct((ti, ch, tj)...  7.06 us

profile of v1, /device:TPU:97, one launch (start us, length us, event | category | flops | bytes accessed | tf_op | source)
XLA Modules:
  0.0 122.1 jit_solution(8918018950006379433)
XLA Ops:
  0.0 36.4 %gather.1 = (bf16[8,512,128]{2,1,0:T(8,128)(2,1)}, bf16[4,4,512,128]{3,2,1,0:T(8,128)(2,1)}) custom-call(bf16[64,64,128]{2,1,0:T(8,128)(2,1)} %bitcast.6, f32[1,64]{1,0:T(1,128)} %bitcast.10, f32[1,64]{1,0:T(1,128)} %bitcast.11, bf16[4,64]{1,0:T(4,128)(2,1)} %bitcast.9), custom_call_target="tpu_custom_call" | custom-call | tf_op jit(solution)/shard_map/gather/pallas_call | solution.py:279
  36.4 61.2 %attend.1.g_ref = bf16[8,512,128]{2,1,0:T(8,128)(2,1)} custom-call(bf16[8,512,128]{2,1,0:T(8,128)(2,1)} %get-tuple-element.7.a_ref, bf16[4,4,512,128]{3,2,1,0:T(8,128)(2,1)} %get-tuple-element.8.bias_ref, s32[1,512]{1,0:T(1,128)} %bitcast.8, bf16[64,64]{1,0:T(8,128)(2,1)} %wq_ref.1, bf16[64,64]{1,0:T(8,128)(2,1)} %wk_ref.1, bf16[64,64]{1,0:T(8,128)(2,1)} %wv_ref.1, ...), custom_call_target="tpu_custom_call" | custom-call | tf_op jit(solution)/shard_map/attend/pallas_call | solution.py:293
  97.6 17.4 %back.1.g_ref = bf16[8,8,64,128]{3,2,1,0:T(8,128)(2,1)} custom-call(bf16[8,512,128]{2,1,0:T(8,128)(2,1)} %attend.1.g_ref), custom_call_target="tpu_custom_call" | custom-call | tf_op jit(solution)/shard_map/back/pallas_call | solution.py:308
  115.0 7.1 %finish.1 = bf16[64,64,128]{2,1,0:T(8,128)(2,1)} custom-call(bf16[8,8,64,128]{3,2,1,0:T(8,128)(2,1)} %back.1.g_ref, bf16[64,64,128]{2,1,0:T(8,128)(2,1)} %bitcast.7, bf16[64,64]{1,0:T(8,128)(2,1)} %wo_ref.1), custom_call_target="tpu_custom_call" | custom-call | tf_op jit(solution)/shard_map/finish/pallas_call | solution.py:317

commit v2 on v1

v2 whole, which is shorter than its diff:
```python
import functools
import math

import jax
import jax.numpy as jnp
import numpy as np
from jax import lax
from jax.experimental import pallas as pl
from jax.experimental.pallas import tpu as pltpu
from jax.sharding import PartitionSpec as P

LN_EPS = 1e-5
MASK_FILL = -1e9
MESH = pl.DeviceIdType.MESH
F32, BF16 = jnp.float32, jnp.bfloat16
NT = (((1,), (1,)), ((), ()))
PAD = 8


def mm(a, b):
    return jnp.dot(a, b, preferred_element_type=F32)


def mm_nt(a, b):
    return lax.dot_general(a, b, NT, preferred_element_type=F32)


def tr(w):
    return jnp.transpose(w.astype(F32)).astype(BF16)


def block_diag2(w):
    z = jnp.zeros_like(w)
    return jnp.concatenate([jnp.concatenate([w, z], 1), jnp.concatenate([z, w], 1)], 0)


def remote(src, dst, send, recv, dev):
    return pltpu.make_async_remote_copy(src_ref=src, dst_ref=dst, send_sem=send, recv_sem=recv, device_id=dev, device_id_type=MESH)


def fill_terms():
    rest, terms = MASK_FILL, []
    for _ in range(3):
        t = float(np.asarray(rest, dtype=BF16))
        terms.append(t)
        rest -= t
    return terms


def pair_rows(wt, e):
    z = jnp.zeros_like(wt)
    lo, hi = jnp.concatenate([wt, z], 1), jnp.concatenate([z, wt], 1)
    return [blk for r in range(0, wt.shape[0], e) for blk in (lo[r:r + e], hi[r:r + e])]


def triangle_kernel(rows, cols, z_ref, gamma_ref, beta_ref, wb_ref, mask_ref, wq_ref, wk_ref, wv_ref, wg_ref, out_ref,
                    stage, bsc, send, a_ref, bias_ref, qp, vt, gt, kh, ss, mm_s, ga, outb, a_sem, x_sem, y_sem, f_sem, o_sem):
    ti, ch, tj = z_ref.shape
    heads = wb_ref.shape[0]
    hj, n, lanes = a_ref.shape
    e = wq_ref.shape[1] // heads
    e2 = 2 * e
    proj2 = 2 * heads * e
    q_scale = 1.0 / math.sqrt(e)
    pitch = rows * hj + PAD
    per_blk = tj // ti
    me_r, me_c = lax.axis_index('row'), lax.axis_index('col')
    core = me_r % 2
    partner = me_r + 1 - 2 * core
    chip = me_r // 2

    barrier = pltpu.get_barrier_semaphore()
    for d in range(1, rows):
        pl.semaphore_signal(barrier, inc=1, device_id={'row': (me_r + d) % rows}, device_id_type=MESH)
    for d in range(1, cols):
        pl.semaphore_signal(barrier, inc=1, device_id={'col': (me_c + d) % cols}, device_id_type=MESH)

    gam = jnp.transpose(jnp.broadcast_to(gamma_ref[...], (tj, ch)))
    bet = jnp.transpose(jnp.broadcast_to(beta_ref[...], (tj, ch)))
    group = 4
    wb = wb_ref[...].astype(F32)
    wb16 = jnp.concatenate([wb] * group, 0)
    wb16 = jnp.concatenate([wb16] * group, 1)
    r_id = lax.broadcasted_iota(jnp.int32, wb16.shape, 0) // heads
    c_id = lax.broadcasted_iota(jnp.int32, wb16.shape, 1) // ch
    wb16 = jnp.where(r_id == c_id, wb16, 0.0).astype(BF16)
    unroll = 2

    def norm_step(t, _):
        for u in range(unroll):
            i0 = (t * unroll + u) * group
            x = z_ref[pl.ds(i0, group)].astype(F32)
            mean = jnp.sum(x, axis=1, keepdims=True) * (1.0 / ch)
            cen = x - mean
            var = jnp.sum(cen * cen, axis=1, keepdims=True) * (1.0 / ch)
            nrm = cen * lax.rsqrt(var + LN_EPS) * gam + bet
            bsc[pl.ds(pl.multiple_of(i0 * heads, group * heads), group * heads), :] = mm(wb16, nrm.astype(BF16).reshape(group * ch, tj))
            for q in range(group):
                t4 = jnp.transpose(nrm[q]).reshape(rows, 2, hj, ch)
                packed = jnp.concatenate([t4[:, 0], t4[:, 1]], axis=-1).reshape(rows * hj, 2 * ch)
                stage[pl.ds(pl.multiple_of((i0 + q) * pitch, 8), rows * hj), :] = packed
        return 0

    lax.fori_loop(0, ti // group // unroll, norm_step, 0)

    my_rows = pl.ds(pl.multiple_of(me_r * ti, ti), ti)
    for h in range(heads):
        bias_ref[me_c, h, my_rows, :] = bsc[pl.ds(h, ti, stride=heads), :].astype(BF16)

    def x_copy(d, src_row):
        rs = pl.ds(pl.multiple_of(src_row * ti, ti), ti)
        return remote(bias_ref.at[me_c, :, rs, :], bias_ref.at[me_c, :, rs, :], x_sem.at[0, d], x_sem.at[1, d], {'row': (me_r + d) % rows})

    def a_copy(d, dst_row, src_row):
        rs = pl.ds(pl.multiple_of(src_row * ti, ti), ti)
        return remote(send.at[dst_row], a_ref.at[:, rs, :], a_sem.at[0, d], a_sem.at[1, d], {'row': (me_r + d) % rows})

    def piece(dst_row, jp):
        return stage[pl.ds(dst_row * hj + jp, ti, stride=pitch), :].astype(BF16)

    hh = heads // 2
    mine, other = pl.ds(core * hh, hh), pl.ds((1 - core) * hh, hh)

    def y_copy(d, blk):
        return remote(bias_ref.at[blk, mine], bias_ref.at[blk, mine], y_sem.at[0, d], y_sem.at[1, d], {'col': (me_c + d) % cols})

    def f_copy(d, blk, part):
        return remote(bias_ref.at[blk, part], bias_ref.at[blk, part], f_sem.at[0, d], f_sem.at[1, d], {'row': partner})

    order = [4, 3, 5, 2, 6, 1, 7] if rows == 8 else list(range(1, rows))
    y_order = [2, 1, 3] if cols == 4 else list(range(1, cols))

    pl.semaphore_wait(barrier, rows + cols - 2)
    for d in order:
        x_copy(d, me_r).start()
    last = None
    for d in order:
        dst = (me_r + d) % rows
        for jp in range(hj):
            send[dst, jp] = piece(dst, jp)
        if last is not None:
            last.start()
        last = a_copy(d, dst, me_r)
    for jp in range(hj):
        a_ref[jp, my_rows, :] = piece(me_r, jp)
    last.start()

    w_qvg = jnp.concatenate(pair_rows(tr(wq_ref[...]), e) + pair_rows(tr(wv_ref[...]), e) + pair_rows(tr(wg_ref[...]), e), 0)
    k_rows = pair_rows(tr(wk_ref[...]), e)
    k_pad = jnp.zeros((lanes - e2, lanes), BF16)
    w_kh = jnp.concatenate([b for h in range(heads) for b in (k_rows[2 * h], k_rows[2 * h + 1], k_pad)], 0)
    masked = jnp.broadcast_to(mask_ref[...] == 0, (lanes, n))
    lane_row = lax.broadcasted_iota(jnp.int32, (lanes, n), 0)
    fill = jnp.zeros((lanes, n), F32)
    for t, f in enumerate(fill_terms()):
        fill = jnp.where(masked & (lane_row == e2 + t), f, fill)
    fill_col = jnp.transpose(fill)
    row_id = lax.broadcasted_iota(jnp.int32, (e, 2 * tj), 0)
    ones_rows = jnp.where(row_id < 3, 1.0, 0.0).astype(BF16)
    eye_r = lax.broadcasted_iota(jnp.int32, (tj, 2 * tj), 0)
    eye_c = lax.broadcasted_iota(jnp.int32, (tj, 2 * tj), 1)
    eye2 = jnp.where(eye_r == lax.rem(eye_c, tj), 1.0, 0.0).astype(BF16)
    z16 = jnp.zeros((e, tj), BF16)
    z_rows = jnp.zeros((lanes - 3 * e, 2 * tj), BF16)

    for d in order:
        x_copy(d, (me_r + rows - d) % rows).wait_recv()
    for d in y_order:
        y_copy(d, me_c).start()
    for d in order:
        a_copy(d, me_r, (me_r + rows - d) % rows).wait_recv()

    def proj_step(jp, _):
        a = a_ref[jp]
        r = mm_nt(w_qvg, a)
        q = (r[:proj2] * q_scale).astype(BF16)
        g = jax.nn.sigmoid(r[2 * proj2:])
        vt[jp] = r[proj2:2 * proj2].astype(BF16)
        for ib in range(cols):
            ls = slice(ib * tj, (ib + 1) * tj)
            gt[jp, ib] = g[:, ls]
            for h in range(heads):
                qp[jp, ib, h, 0:e, 0:tj] = q[h * e2:h * e2 + e, ls]
                qp[jp, ib, h, 0:e, tj:2 * tj] = z16
                qp[jp, ib, h, e:e2, 0:tj] = z16
                qp[jp, ib, h, e:e2, tj:2 * tj] = q[h * e2 + e:h * e2 + e2, ls]
                qp[jp, ib, h, e2:3 * e, :] = ones_rows
        k = mm_nt(a, w_kh)
        for h in range(heads):
            kh[jp, h] = (k[:, h * lanes:(h + 1) * lanes] + fill_col).astype(BF16)
        return 0

    lax.fori_loop(0, hj, proj_step, 0)

    away = [2, 1, 3, 0] if cols == 4 else [(k + 1) % cols for k in range(cols)]
    shift = (me_c - chip + cols) % cols
    pos = sum(jnp.where(shift == a, k, 0) for k, a in enumerate(away))

    def block_of(phase):
        k = jnp.where(phase <= pos, phase - 1, phase)
        step = sum(jnp.where(k == i, a, 0) for i, a in enumerate(away))
        return jnp.where(phase == 0, me_c, (chip + step) % cols)

    halves = 2
    ck = n // halves

    def scores_steps(ib, jp, h, slot):
        rhs = jnp.concatenate([qp[jp, ib, h], z_rows, eye2], 0)
        mx = jnp.full((8, 2 * tj), -jnp.inf, F32)
        for c in range(halves):
            rs = slice(c * ck, (c + 1) * ck)
            s = mm(jnp.concatenate([kh[jp, h, rs], bias_ref[ib, h, rs]], 1), rhs)
            ss[slot, rs] = s
            mx = jnp.maximum(mx, jnp.max(s.reshape(ck // 8, 8, 2 * tj), axis=0))
            if c == halves - 1:
                mm_s[slot] = jnp.max(mx, axis=0, keepdims=True)
            yield

    def softmax_steps(ib, jp, h, slot):
        l = jnp.zeros((8, 2 * tj), F32)
        m = mm_s[slot]
        o = jnp.zeros((e2, 2 * tj), F32)
        for c in range(halves):
            rs = slice(c * ck, (c + 1) * ck)
            p = jnp.exp(ss[slot, rs] - m)
            l = l + jnp.sum(p.reshape(ck // 8, 8, 2 * tj), axis=0)
            o = o + mm(vt[jp, h * e2:(h + 1) * e2, rs], p.astype(BF16))
            if c == halves - 1:
                l1 = jnp.sum(l, axis=0, keepdims=True)
                for half in range(2):
                    ls = slice(half * tj, (half + 1) * tj)
                    r2 = slice(h * e2 + half * e, h * e2 + (half + 1) * e)
                    ga[r2, :] = gt[jp, ib, r2, :] * (o[half * e:(half + 1) * e, ls] / l1[:, ls])
            yield

    def out_copy(dst_row, src_jp, slot, slot_jp):
        rs = pl.ds(pl.multiple_of(dst_row * ti, ti), ti)
        return remote(outb.at[src_jp, rs, :], out_ref.at[slot, slot_jp], o_sem.at[0, dst_row], o_sem.at[1, slot], {'row': dst_row})

    def send_out(t):
        ib, jp = block_of(t // hj), t % hj
        for k in range(per_blk):
            dst_row = ib * per_blk + k

            @pl.when(dst_row != me_r)
            def _():
                out_copy(dst_row, jp, me_r, jp).start()

            @pl.when(dst_row == me_r)
            def _():
                out_ref[me_r, jp] = outb[jp, my_rows, :]

    for _ in scores_steps(block_of(0), 0, 0, 0):
        pass

    units = cols * hj

    def unit(t, _):
        for phase in range(1, cols):
            @pl.when(t == phase * hj - 4)
            def _():
                blk = block_of(phase)
                d = (me_c - blk + cols) % cols
                y_copy(d, blk).wait_recv()
                f_copy(d, blk, mine).start()

            @pl.when(t == phase * hj - 1)
            def _():
                blk = block_of(phase)
                d = (me_c - blk + cols) % cols
                f_copy(d, blk, other).wait_recv()

        @pl.when(t > 0)
        def _():
            send_out(t - 1)

        ib, jp = block_of(t // hj), t % hj
        t_next = (t + 1) % units
        ib_next, jp_next = block_of(t_next // hj), t_next % hj
        for h in range(heads):
            nxt = (ib, jp, h + 1) if h + 1 < heads else (ib_next, jp_next, 0)
            for _ in zip(scores_steps(*nxt, (h + 1) % 2), softmax_steps(ib, jp, h, h % 2)):
                pass
        outb[jp, pl.ds(pl.multiple_of(ib * tj, tj), tj), :] = jnp.transpose(ga[...]).astype(BF16)
        return 0

    lax.fori_loop(0, units, unit, 0)
    send_out(units - 1)

    for d in order:
        x_copy(d, me_r).wait_send()
        a_copy(d, (me_r + d) % rows, me_r).wait_send()
    for d in y_order:
        y_copy(d, me_c).wait_send()
        f_copy(d, me_c, mine).wait_send()

    def all_out(send_row, slot):
        rs = pl.ds(pl.multiple_of(send_row * ti, ti), ti)
        return remote(outb.at[:, rs, :], out_ref.at[slot], o_sem.at[0, send_row], o_sem.at[1, slot], {'row': partner})

    for d in order:
        src = (me_r + rows - d) % rows
        all_out(src, src).wait_recv()
    for d in order:
        dst = (me_r + d) % rows
        all_out(dst, dst).wait_send()


def finish_kernel(e, g_ref, z_ref, wo_ref, out_ref, stage):
    rows, hj, ti, lanes = g_ref.shape
    ch, tj = z_ref.shape[1:]
    pitch = ti + PAD
    n_rj = rows * hj
    wo = wo_ref[...].astype(F32)
    z = jnp.zeros((e, ch), F32)
    wo = tr(jnp.concatenate([blk for r in range(0, wo.shape[0], e) for blk in (wo[r:r + e], z)], 0))

    def widen(t, _):
        for jp in range(hj):
            stage[pl.ds(pl.multiple_of((t * hj + jp) * pitch, 8), ti), :] = g_ref[t, jp].astype(F32)
        return 0

    lax.fori_loop(0, rows, widen, 0)

    group = 8

    def step(t, _):
        for q in range(group):
            i = t * group + q
            x = stage[pl.ds(i, n_rj, stride=pitch), :]
            y = pltpu.roll(x, lanes - e, 1)
            x2 = jnp.concatenate([x.reshape(rows, 1, hj, lanes), y.reshape(rows, 1, hj, lanes)], 1).reshape(tj, lanes).astype(BF16)
            out_ref[i] = (mm_nt(wo, x2) + z_ref[i].astype(F32)).astype(BF16)
        return 0

    lax.fori_loop(0, ti // group, step, 0)


VM = pl.BlockSpec(memory_space=pltpu.VMEM)


def solution(mesh):
    rows, cols = mesh.shape['row'], mesh.shape['col']

    def body(pair_tile, res_mask, ln_gamma, ln_beta, w_q, w_k, w_v, w_b, w_g, w_o):
        ti, tj, ch = pair_tile.shape
        heads = w_b.shape[1]
        proj = w_q.shape[1]
        n = ti * rows
        hj = tj // rows // 2
        z = jnp.transpose(pair_tile, (0, 2, 1))
        dma = pltpu.SemaphoreType.DMA
        e = proj // heads
        back = pl.pallas_call(
            functools.partial(triangle_kernel, rows, cols),
            out_shape=jax.ShapeDtypeStruct((rows, hj, ti, 2 * ch), BF16),
            in_specs=[VM] * 9,
            out_specs=VM,
            scratch_shapes=[
                pltpu.VMEM((ti * (rows * hj + PAD), 2 * ch), F32),
                pltpu.VMEM((ti * heads, tj), F32),
                pltpu.VMEM((rows, hj, ti, 2 * ch), BF16),
                pltpu.VMEM((hj, n, 2 * ch), BF16),
                pltpu.VMEM((cols, heads, n, tj), BF16),
                pltpu.VMEM((hj, cols, heads, 3 * e, 2 * tj), BF16),
                pltpu.VMEM((hj, 2 * proj, n), BF16),
                pltpu.VMEM((hj, cols, 2 * proj, tj), F32),
                pltpu.VMEM((hj, heads, n, 2 * ch), BF16),
                pltpu.VMEM((2, n, 2 * tj), F32),
                pltpu.VMEM((2, 1, 2 * tj), F32),
                pltpu.VMEM((2 * proj, tj), F32),
                pltpu.VMEM((hj, n, 2 * proj), BF16),
                dma((2, rows)), dma((2, rows)), dma((2, cols)), dma((2, cols)), dma((2, rows)),
            ],
            compiler_params=pltpu.CompilerParams(collective_id=0, has_side_effects=True),
            name='triangle',
        )(z, ln_gamma.reshape(1, ch), ln_beta.reshape(1, ch), w_b.T, res_mask.reshape(1, n), w_q, w_k, w_v, w_g)
        out = pl.pallas_call(
            functools.partial(finish_kernel, proj // heads),
            out_shape=jax.ShapeDtypeStruct((ti, ch, tj), BF16),
            in_specs=[VM] * 3,
            out_specs=VM,
            scratch_shapes=[pltpu.VMEM((rows * hj * (ti + PAD), 2 * ch), F32)],
            name='finish',
        )(back, z, w_o)
        return jnp.transpose(out, (0, 2, 1))

    tile_spec = P(('data', 'row'), 'col', None)
    return jax.shard_map(body, mesh=mesh, in_specs=(tile_spec, P('data'), P(), P(), P(), P(), P(), P(), P(), P()), out_specs=tile_spec, check_vma=False)
```

time: 122 us -> 72.1 us (0.59); the launches traced: 122 us -> 70.8 us
  Pallas kernels: 122 us -> 70.8 us
    pallas_call x4 -> x2, Pallas kernels: 122 us -> 70.8 us  [the longest x1 65.2 us: body(): pl.pallas_call(functools.partial(triangle_kernel, rows, cols), out_shape=...]
where the time goes in v2:
time: 72.1 us; the launch traced here: 70.8 us
  Pallas kernels  70.8 us (98%)
    pallas_call x1, Pallas kernels, body(): pl.pallas_call(functools.partial(triangle_kernel, rows, cols), out_shape=...  65.2 us
    pallas_call x1, Pallas kernels, body(): pl.pallas_call(functools.partial(finish_kernel, proj // heads), out_shape...  5.61 us

profile of v2, /device:TPU:97, one launch (start us, length us, event | category | flops | bytes accessed | tf_op | source)
XLA Modules:
  0.0 70.8 jit_solution(15055274327842384367)
XLA Ops:
  0.0 65.2 %triangle.1.g_ref = bf16[8,8,64,128]{3,2,1,0:T(8,128)(2,1)} custom-call(bf16[64,64,128]{2,1,0:T(8,128)(2,1)} %bitcast.6, f32[1,64]{1,0:T(1,128)} %bitcast.10, f32[1,64]{1,0:T(1,128)} %bitcast.11, bf16[4,64]{1,0:T(4,128)(2,1)} %bitcast.9, s32[1,512]{1,0:T(1,128)} %bitcast.8, bf16[64,64]{1,0:T(8,128)(2,1)} %wq_ref.1, bf16[64,64]{1,0:T(8,128)(2,1)} %wk_ref.1, ...), custom_call_target="tpu_custom_call" | custom-call | tf_op jit(solution)/shard_map/triangle/pallas_call | solution.py:354
  65.2 5.6 %finish.1 = bf16[64,64,128]{2,1,0:T(8,128)(2,1)} custom-call(bf16[8,8,64,128]{3,2,1,0:T(8,128)(2,1)} %triangle.1.g_ref, bf16[64,64,128]{2,1,0:T(8,128)(2,1)} %bitcast.7, bf16[64,64]{1,0:T(8,128)(2,1)} %wo_ref.1), custom_call_target="tpu_custom_call" | custom-call | tf_op jit(solution)/shard_map/finish/pallas_call | solution.py:378

commit v3 on v2

--- a/solution.py
+++ b/solution.py
@@ -54,7 +54,7 @@
 
 
 def triangle_kernel(rows, cols, z_ref, gamma_ref, beta_ref, wb_ref, mask_ref, wq_ref, wk_ref, wv_ref, wg_ref, out_ref,
-                    stage, bsc, send, a_ref, bias_ref, qp, vt, gt, kh, ss, mm_s, ga, outb, a_sem, x_sem, y_sem, f_sem, o_sem):
+                    stage, bsc, bown, send, a_ref, bias_ref, qp, vt, gt, kh, ss, mm_s, ga, outb, a_sem, x_sem, y_sem, f_sem, o_sem):
     ti, ch, tj = z_ref.shape
     heads = wb_ref.shape[0]
     hj, n, lanes = a_ref.shape
@@ -104,23 +104,24 @@
     lax.fori_loop(0, ti // group // unroll, norm_step, 0)
 
     my_rows = pl.ds(pl.multiple_of(me_r * ti, ti), ti)
+    hh = heads // 2
+    mine, other = pl.ds(core * hh, hh), pl.ds((1 - core) * hh, hh)
     for h in range(heads):
-        bias_ref[me_c, h, my_rows, :] = bsc[pl.ds(h, ti, stride=heads), :].astype(BF16)
-
-    def x_copy(d, src_row):
+        bown[h] = bsc[pl.ds(h, ti, stride=heads), :].astype(BF16)
+    bias_ref[me_c, mine, my_rows, :] = bown[mine]
+
+    def x_copy(d, dst_row, src_row):
         rs = pl.ds(pl.multiple_of(src_row * ti, ti), ti)
-        return remote(bias_ref.at[me_c, :, rs, :], bias_ref.at[me_c, :, rs, :], x_sem.at[0, d], x_sem.at[1, d], {'row': (me_r + d) % rows})
-
-    def a_copy(d, dst_row, src_row):
+        part = pl.ds((dst_row % 2) * hh, hh)
+        return remote(bown.at[part], bias_ref.at[me_c, part, rs, :], x_sem.at[0, d], x_sem.at[1, d], {'row': (me_r + d) % rows})
+
+    def a_copy(d, jp, dst_row, src_row):
         rs = pl.ds(pl.multiple_of(src_row * ti, ti), ti)
-        return remote(send.at[dst_row], a_ref.at[:, rs, :], a_sem.at[0, d], a_sem.at[1, d], {'row': (me_r + d) % rows})
+        return remote(send.at[dst_row, jp], a_ref.at[jp, rs, :], a_sem.at[0, jp, d], a_sem.at[1, jp, d], {'row': (me_r + d) % rows})
 
     def piece(dst_row, jp):
         return stage[pl.ds(dst_row * hj + jp, ti, stride=pitch), :].astype(BF16)
 
-    hh = heads // 2
-    mine, other = pl.ds(core * hh, hh), pl.ds((1 - core) * hh, hh)
-
     def y_copy(d, blk):
         return remote(bias_ref.at[blk, mine], bias_ref.at[blk, mine], y_sem.at[0, d], y_sem.at[1, d], {'col': (me_c + d) % cols})
 
@@ -132,18 +133,16 @@
 
     pl.semaphore_wait(barrier, rows + cols - 2)
     for d in order:
-        x_copy(d, me_r).start()
-    last = None
-    for d in order:
-        dst = (me_r + d) % rows
-        for jp in range(hj):
-            send[dst, jp] = piece(dst, jp)
-        if last is not None:
-            last.start()
-        last = a_copy(d, dst, me_r)
-    for jp in range(hj):
-        a_ref[jp, my_rows, :] = piece(me_r, jp)
-    last.start()
+        x_copy(d, (me_r + d) % rows, me_r).start()
+    for jp in range(hj + 1):
+        if jp < hj:
+            for d in order:
+                dst = (me_r + d) % rows
+                send[dst, jp] = piece(dst, jp)
+            a_ref[jp, my_rows, :] = piece(me_r, jp)
+        if jp > 0:
+            for d in order:
+                a_copy(d, jp - 1, (me_r + d) % rows, me_r).start()
 
     w_qvg = jnp.concatenate(pair_rows(tr(wq_ref[...]), e) + pair_rows(tr(wv_ref[...]), e) + pair_rows(tr(wg_ref[...]), e), 0)
     k_rows = pair_rows(tr(wk_ref[...]), e)
@@ -164,13 +163,16 @@
     z_rows = jnp.zeros((lanes - 3 * e, 2 * tj), BF16)
 
     for d in order:
-        x_copy(d, (me_r + rows - d) % rows).wait_recv()
+        x_copy(d, me_r, (me_r + rows - d) % rows).wait_recv()
+    f_copy(0, me_c, mine).start()
     for d in y_order:
         y_copy(d, me_c).start()
-    for d in order:
-        a_copy(d, me_r, (me_r + rows - d) % rows).wait_recv()
-
-    def proj_step(jp, _):
+
+    def wait_cols(jp):
+        for d in order:
+            a_copy(d, jp, me_r, (me_r + rows - d) % rows).wait_recv()
+
+    def project(jp):
         a = a_ref[jp]
         r = mm_nt(w_qvg, a)
         q = (r[:proj2] * q_scale).astype(BF16)
@@ -188,9 +190,6 @@
         k = mm_nt(a, w_kh)
         for h in range(heads):
             kh[jp, h] = (k[:, h * lanes:(h + 1) * lanes] + fill_col).astype(BF16)
-        return 0
-
-    lax.fori_loop(0, hj, proj_step, 0)
 
     away = [2, 1, 3, 0] if cols == 4 else [(k + 1) % cols for k in range(cols)]
     shift = (me_c - chip + cols) % cols
@@ -250,30 +249,9 @@
             def _():
                 out_ref[me_r, jp] = outb[jp, my_rows, :]
 
-    for _ in scores_steps(block_of(0), 0, 0, 0):
-        pass
-
     units = cols * hj
 
-    def unit(t, _):
-        for phase in range(1, cols):
-            @pl.when(t == phase * hj - 4)
-            def _():
-                blk = block_of(phase)
-                d = (me_c - blk + cols) % cols
-                y_copy(d, blk).wait_recv()
-                f_copy(d, blk, mine).start()
-
-            @pl.when(t == phase * hj - 1)
-            def _():
-                blk = block_of(phase)
-                d = (me_c - blk + cols) % cols
-                f_copy(d, blk, other).wait_recv()
-
-        @pl.when(t > 0)
-        def _():
-            send_out(t - 1)
-
+    def attend(t):
         ib, jp = block_of(t // hj), t % hj
         t_next = (t + 1) % units
         ib_next, jp_next = block_of(t_next // hj), t_next % hj
@@ -282,16 +260,59 @@
             for _ in zip(scores_steps(*nxt, (h + 1) % 2), softmax_steps(ib, jp, h, h % 2)):
                 pass
         outb[jp, pl.ds(pl.multiple_of(ib * tj, tj), tj), :] = jnp.transpose(ga[...]).astype(BF16)
+
+    wait_cols(0)
+    project(0)
+    f_copy(0, me_c, other).wait_recv()
+    for _ in scores_steps(block_of(0), 0, 0, 0):
+        pass
+
+    def first_unit(t, _):
+        wait_cols(t + 1)
+        project(t + 1)
+
+        @pl.when(t > 0)
+        def _():
+            send_out(t - 1)
+
+        attend(t)
         return 0
 
-    lax.fori_loop(0, units, unit, 0)
+    lax.fori_loop(0, hj - 1, first_unit, 0)
+
+    def unit(t, _):
+        for phase in range(1, cols):
+            @pl.when(t == phase * hj - 1)
+            def _():
+                blk = block_of(phase)
+                d = (me_c - blk + cols) % cols
+                f_copy(d, blk, other).wait_recv()
+
+            if phase + 1 < cols:
+                @pl.when(t == (phase + 1) * hj - 4)
+                def _():
+                    blk = block_of(phase + 1)
+                    d = (me_c - blk + cols) % cols
+                    y_copy(d, blk).wait_recv()
+                    f_copy(d, blk, mine).start()
+
+        send_out(t - 1)
+        attend(t)
+        return 0
+
+    blk = block_of(1)
+    y_copy((me_c - blk + cols) % cols, blk).wait_recv()
+    f_copy((me_c - blk + cols) % cols, blk, mine).start()
+    lax.fori_loop(hj - 1, units, unit, 0)
     send_out(units - 1)
 
     for d in order:
-        x_copy(d, me_r).wait_send()
-        a_copy(d, (me_r + d) % rows, me_r).wait_send()
+        x_copy(d, (me_r + d) % rows, me_r).wait_send()
+        for jp in range(hj):
+            a_copy(d, jp, (me_r + d) % rows, me_r).wait_send()
     for d in y_order:
         y_copy(d, me_c).wait_send()
+    for d in range(cols):
         f_copy(d, me_c, mine).wait_send()
 
     def all_out(send_row, slot):
@@ -359,6 +380,7 @@
             scratch_shapes=[
                 pltpu.VMEM((ti * (rows * hj + PAD), 2 * ch), F32),
                 pltpu.VMEM((ti * heads, tj), F32),
+                pltpu.VMEM((heads, ti, tj), BF16),
                 pltpu.VMEM((rows, hj, ti, 2 * ch), BF16),
                 pltpu.VMEM((hj, n, 2 * ch), BF16),
                 pltpu.VMEM((cols, heads, n, tj), BF16),
@@ -370,7 +392,7 @@
                 pltpu.VMEM((2, 1, 2 * tj), F32),
                 pltpu.VMEM((2 * proj, tj), F32),
                 pltpu.VMEM((hj, n, 2 * proj), BF16),
-                dma((2, rows)), dma((2, rows)), dma((2, cols)), dma((2, cols)), dma((2, rows)),
+                dma((2, hj, rows)), dma((2, rows)), dma((2, cols)), dma((2, cols)), dma((2, rows)),
             ],
             compiler_params=pltpu.CompilerParams(collective_id=0, has_side_effects=True),
             name='triangle',

time: 72.1 us -> 64.5 us (0.89); the launches traced: 70.8 us -> 64.4 us
  Pallas kernels: 70.8 us -> 64.4 us
    pallas_call x1, Pallas kernels: 65.2 us -> 58.8 us  [body(): pl.pallas_call(functools.partial(triangle_kernel, rows, cols), out_shape=...]
where the time goes in v3:
time: 64.5 us; the launch traced here: 64.4 us
  Pallas kernels  64.4 us (100%)
    pallas_call x1, Pallas kernels, body(): pl.pallas_call(functools.partial(triangle_kernel, rows, cols), out_shape=...  58.8 us
    pallas_call x1, Pallas kernels, body(): pl.pallas_call(functools.partial(finish_kernel, proj // heads), out_shape...  5.61 us

profile of v3, /device:TPU:97, one launch (start us, length us, event | category | flops | bytes accessed | tf_op | source)
XLA Modules:
  0.0 64.4 jit_solution(564451545459935609)
XLA Ops:
  0.0 58.8 %triangle.1.g_ref = bf16[8,8,64,128]{3,2,1,0:T(8,128)(2,1)} custom-call(bf16[64,64,128]{2,1,0:T(8,128)(2,1)} %bitcast.6, f32[1,64]{1,0:T(1,128)} %bitcast.10, f32[1,64]{1,0:T(1,128)} %bitcast.11, bf16[4,64]{1,0:T(4,128)(2,1)} %bitcast.9, s32[1,512]{1,0:T(1,128)} %bitcast.8, bf16[64,64]{1,0:T(8,128)(2,1)} %wq_ref.1, bf16[64,64]{1,0:T(8,128)(2,1)} %wk_ref.1, ...), custom_call_target="tpu_custom_call" | custom-call | tf_op jit(solution)/shard_map/triangle/pallas_call | solution.py:375
  58.8 5.6 %finish.1 = bf16[64,64,128]{2,1,0:T(8,128)(2,1)} custom-call(bf16[8,8,64,128]{3,2,1,0:T(8,128)(2,1)} %triangle.1.g_ref, bf16[64,64,128]{2,1,0:T(8,128)(2,1)} %bitcast.7, bf16[64,64]{1,0:T(8,128)(2,1)} %wo_ref.1), custom_call_target="tpu_custom_call" | custom-call | tf_op jit(solution)/shard_map/finish/pallas_call | solution.py:400

commit v4 on v3

--- a/solution.py
+++ b/solution.py
@@ -54,7 +54,7 @@
 
 
 def triangle_kernel(rows, cols, z_ref, gamma_ref, beta_ref, wb_ref, mask_ref, wq_ref, wk_ref, wv_ref, wg_ref, out_ref,
-                    stage, bsc, bown, send, a_ref, bias_ref, qp, vt, gt, kh, ss, mm_s, ga, outb, a_sem, x_sem, y_sem, f_sem, o_sem):
+                    stage, bsc, bown, send, a_ref, bias_ref, qp, vt, gt, kh, ss, mm_s, lp, os_, outb, a_sem, x_sem, y_sem, f_sem, o_sem):
     ti, ch, tj = z_ref.shape
     heads = wb_ref.shape[0]
     hj, n, lanes = a_ref.shape
@@ -202,35 +202,42 @@
 
     halves = 2
     ck = n // halves
-
-    def scores_steps(ib, jp, h, slot):
+    slots = heads
+
+    def scores_dot(ib, jp, h):
         rhs = jnp.concatenate([qp[jp, ib, h], z_rows, eye2], 0)
-        mx = jnp.full((8, 2 * tj), -jnp.inf, F32)
+        return jnp.concatenate([mm(jnp.concatenate([kh[jp, h, c * ck:(c + 1) * ck], bias_ref[ib, h, c * ck:(c + 1) * ck]], 1), rhs) for c in range(halves)], 0)
+
+    def drain(s, c, slot, mx):
+        part = s[c * ck:(c + 1) * ck]
+        ss[slot, c * ck:(c + 1) * ck] = part
+        part = jnp.max(part.reshape(ck // 8, 8, 2 * tj), axis=0)
+        return part if mx is None else jnp.maximum(mx, part)
+
+    def weigh(jp, h, slot, c, l, o):
+        rs = slice(c * ck, (c + 1) * ck)
+        p = jnp.exp(ss[slot, rs] - mm_s[slot])
+        part = jnp.sum(p.reshape(ck // 8, 8, 2 * tj), axis=0)
+        ob = mm(vt[jp, h * e2:(h + 1) * e2, rs], p.astype(BF16))
+        return (part, ob) if l is None else (l + part, o + ob)
+
+    def scores(ib, jp, h):
+        s = scores_dot(ib, jp, h)
+        mx = None
         for c in range(halves):
-            rs = slice(c * ck, (c + 1) * ck)
-            s = mm(jnp.concatenate([kh[jp, h, rs], bias_ref[ib, h, rs]], 1), rhs)
-            ss[slot, rs] = s
-            mx = jnp.maximum(mx, jnp.max(s.reshape(ck // 8, 8, 2 * tj), axis=0))
-            if c == halves - 1:
-                mm_s[slot] = jnp.max(mx, axis=0, keepdims=True)
-            yield
-
-    def softmax_steps(ib, jp, h, slot):
-        l = jnp.zeros((8, 2 * tj), F32)
-        m = mm_s[slot]
-        o = jnp.zeros((e2, 2 * tj), F32)
-        for c in range(halves):
-            rs = slice(c * ck, (c + 1) * ck)
-            p = jnp.exp(ss[slot, rs] - m)
-            l = l + jnp.sum(p.reshape(ck // 8, 8, 2 * tj), axis=0)
-            o = o + mm(vt[jp, h * e2:(h + 1) * e2, rs], p.astype(BF16))
-            if c == halves - 1:
-                l1 = jnp.sum(l, axis=0, keepdims=True)
-                for half in range(2):
-                    ls = slice(half * tj, (half + 1) * tj)
-                    r2 = slice(h * e2 + half * e, h * e2 + (half + 1) * e)
-                    ga[r2, :] = gt[jp, ib, r2, :] * (o[half * e:(half + 1) * e, ls] / l1[:, ls])
-            yield
+            mx = drain(s, c, h, mx)
+        mm_s[h] = jnp.max(mx, axis=0, keepdims=True)
+
+    def finish_unit(t):
+        ib, jp = block_of(t // hj), t % hj
+        parts = []
+        for h in range(heads):
+            l1 = jnp.sum(lp[h], axis=0, keepdims=True)
+            for half in range(2):
+                ls = slice(half * tj, (half + 1) * tj)
+                rs = slice(h * e2 + half * e, h * e2 + (half + 1) * e)
+                parts.append(gt[jp, ib, rs, :] * (os_[h, half * e:(half + 1) * e, ls] / l1[:, ls]))
+        outb[jp, pl.ds(pl.multiple_of(ib * tj, tj), tj), :] = jnp.transpose(jnp.concatenate(parts, 0)).astype(BF16)
 
     def out_copy(dst_row, src_jp, slot, slot_jp):
         rs = pl.ds(pl.multiple_of(dst_row * ti, ti), ti)
@@ -255,25 +262,34 @@
         ib, jp = block_of(t // hj), t % hj
         t_next = (t + 1) % units
         ib_next, jp_next = block_of(t_next // hj), t_next % hj
+        finish_unit(jnp.maximum(t - 1, 0))
         for h in range(heads):
-            nxt = (ib, jp, h + 1) if h + 1 < heads else (ib_next, jp_next, 0)
-            for _ in zip(scores_steps(*nxt, (h + 1) % 2), softmax_steps(ib, jp, h, h % 2)):
-                pass
-        outb[jp, pl.ds(pl.multiple_of(ib * tj, tj), tj), :] = jnp.transpose(ga[...]).astype(BF16)
-
+            nxt = (ib, jp, h + 2) if h + 2 < heads else (ib_next, jp_next, h + 2 - heads)
+            s = scores_dot(*nxt)
+            l, o, mx = None, None, None
+            for c in range(halves):
+                mx = drain(s, c, nxt[2], mx)
+                l, o = weigh(jp, h, h, c, l, o)
+
+            mm_s[nxt[2]] = jnp.max(mx, axis=0, keepdims=True)
+            os_[h] = o
+            lp[h] = l
+
+    os_[...] = jnp.ones_like(os_)
+    lp[...] = jnp.ones_like(lp)
     wait_cols(0)
     project(0)
     f_copy(0, me_c, other).wait_recv()
-    for _ in scores_steps(block_of(0), 0, 0, 0):
-        pass
+    for h in range(2):
+        scores(me_c, 0, h)
 
     def first_unit(t, _):
         wait_cols(t + 1)
         project(t + 1)
 
-        @pl.when(t > 0)
+        @pl.when(t > 1)
         def _():
-            send_out(t - 1)
+            send_out(t - 2)
 
         attend(t)
         return 0
@@ -296,7 +312,7 @@
                     y_copy(d, blk).wait_recv()
                     f_copy(d, blk, mine).start()
 
-        send_out(t - 1)
+        send_out(t - 2)
         attend(t)
         return 0
 
@@ -304,6 +320,8 @@
     y_copy((me_c - blk + cols) % cols, blk).wait_recv()
     f_copy((me_c - blk + cols) % cols, blk, mine).start()
     lax.fori_loop(hj - 1, units, unit, 0)
+    finish_unit(units - 1)
+    send_out(units - 2)
     send_out(units - 1)
 
     for d in order:
@@ -388,9 +406,10 @@
                 pltpu.VMEM((hj, 2 * proj, n), BF16),
                 pltpu.VMEM((hj, cols, 2 * proj, tj), F32),
                 pltpu.VMEM((hj, heads, n, 2 * ch), BF16),
-                pltpu.VMEM((2, n, 2 * tj), F32),
-                pltpu.VMEM((2, 1, 2 * tj), F32),
-                pltpu.VMEM((2 * proj, tj), F32),
+                pltpu.VMEM((heads, n, 2 * tj), F32),
+                pltpu.VMEM((heads, 1, 2 * tj), F32),
+                pltpu.VMEM((heads, 8, 2 * tj), F32),
+                pltpu.VMEM((heads, 2 * e, 2 * tj), F32),
                 pltpu.VMEM((hj, n, 2 * proj), BF16),
                 dma((2, hj, rows)), dma((2, rows)), dma((2, cols)), dma((2, cols)), dma((2, rows)),
             ],

time: 64.5 us -> 58.2 us (0.902)
  Pallas kernels: 64.4 us -> 58.1 us
    pallas_call x1, Pallas kernels: 58.8 us -> 52.5 us  [body(): pl.pallas_call(functools.partial(triangle_kernel, rows, cols), out_shape=...]
where the time goes in v4:
time: 58.2 us; the launch traced here: 58.1 us
  Pallas kernels  58.1 us (100%)
    pallas_call x1, Pallas kernels, body(): pl.pallas_call(functools.partial(triangle_kernel, rows, cols), out_shape=...  52.5 us
    pallas_call x1, Pallas kernels, body(): pl.pallas_call(functools.partial(finish_kernel, proj // heads), out_shape...  5.61 us

profile of v4, /device:TPU:97, one launch (start us, length us, event | category | flops | bytes accessed | tf_op | source)
XLA Modules:
  0.0 58.1 jit_solution(13284103595736288342)
XLA Ops:
  0.0 52.5 %triangle.1.g_ref = bf16[8,8,64,128]{3,2,1,0:T(8,128)(2,1)} custom-call(bf16[64,64,128]{2,1,0:T(8,128)(2,1)} %bitcast.6, f32[1,64]{1,0:T(1,128)} %bitcast.10, f32[1,64]{1,0:T(1,128)} %bitcast.11, bf16[4,64]{1,0:T(4,128)(2,1)} %bitcast.9, s32[1,512]{1,0:T(1,128)} %bitcast.8, bf16[64,64]{1,0:T(8,128)(2,1)} %wq_ref.1, bf16[64,64]{1,0:T(8,128)(2,1)} %wk_ref.1, ...), custom_call_target="tpu_custom_call" | custom-call | tf_op jit(solution)/shard_map/triangle/pallas_call | solution.py:393
  52.5 5.6 %finish.1 = bf16[64,64,128]{2,1,0:T(8,128)(2,1)} custom-call(bf16[8,8,64,128]{3,2,1,0:T(8,128)(2,1)} %triangle.1.g_ref, bf16[64,64,128]{2,1,0:T(8,128)(2,1)} %bitcast.7, bf16[64,64]{1,0:T(8,128)(2,1)} %wo_ref.1), custom_call_target="tpu_custom_call" | custom-call | tf_op jit(solution)/shard_map/finish/pallas_call | solution.py:419

commit v5 on v4

--- a/solution.py
+++ b/solution.py
@@ -54,7 +54,7 @@
 
 
 def triangle_kernel(rows, cols, z_ref, gamma_ref, beta_ref, wb_ref, mask_ref, wq_ref, wk_ref, wv_ref, wg_ref, out_ref,
-                    stage, bsc, bown, send, a_ref, bias_ref, qp, vt, gt, kh, ss, mm_s, lp, os_, outb, a_sem, x_sem, y_sem, f_sem, o_sem):
+                    stage, bsc, bown, send, a_ref, bias_ref, qp, vt, gt, kh, ss, mm_s, lp, os_, outb, a_sem, x_sem, y_sem, f_sem, g_sem, o_sem):
     ti, ch, tj = z_ref.shape
     heads = wb_ref.shape[0]
     hj, n, lanes = a_ref.shape
@@ -84,7 +84,7 @@
     r_id = lax.broadcasted_iota(jnp.int32, wb16.shape, 0) // heads
     c_id = lax.broadcasted_iota(jnp.int32, wb16.shape, 1) // ch
     wb16 = jnp.where(r_id == c_id, wb16, 0.0).astype(BF16)
-    unroll = 2
+    unroll = 4
 
     def norm_step(t, _):
         for u in range(unroll):
@@ -129,7 +129,7 @@
         return remote(bias_ref.at[blk, part], bias_ref.at[blk, part], f_sem.at[0, d], f_sem.at[1, d], {'row': partner})
 
     order = [4, 3, 5, 2, 6, 1, 7] if rows == 8 else list(range(1, rows))
-    y_order = [2, 1, 3] if cols == 4 else list(range(1, cols))
+    y_order = [1, cols - 1]
 
     pl.semaphore_wait(barrier, rows + cols - 2)
     for d in order:
@@ -191,14 +191,7 @@
         for h in range(heads):
             kh[jp, h] = (k[:, h * lanes:(h + 1) * lanes] + fill_col).astype(BF16)
 
-    away = [2, 1, 3, 0] if cols == 4 else [(k + 1) % cols for k in range(cols)]
-    shift = (me_c - chip + cols) % cols
-    pos = sum(jnp.where(shift == a, k, 0) for k, a in enumerate(away))
-
-    def block_of(phase):
-        k = jnp.where(phase <= pos, phase - 1, phase)
-        step = sum(jnp.where(k == i, a, 0) for i, a in enumerate(away))
-        return jnp.where(phase == 0, me_c, (chip + step) % cols)
+    blk_a, blk_b, blk_d = (me_c + 1) % cols, (me_c + cols - 1) % cols, (me_c + 2) % cols
 
     halves = 2
     ck = n // halves
@@ -228,8 +221,7 @@
             mx = drain(s, c, h, mx)
         mm_s[h] = jnp.max(mx, axis=0, keepdims=True)
 
-    def finish_unit(t):
-        ib, jp = block_of(t // hj), t % hj
+    def finish_unit(jp, ib):
         parts = []
         for h in range(heads):
             l1 = jnp.sum(lp[h], axis=0, keepdims=True)
@@ -243,8 +235,7 @@
         rs = pl.ds(pl.multiple_of(dst_row * ti, ti), ti)
         return remote(outb.at[src_jp, rs, :], out_ref.at[slot, slot_jp], o_sem.at[0, dst_row], o_sem.at[1, slot], {'row': dst_row})
 
-    def send_out(t):
-        ib, jp = block_of(t // hj), t % hj
+    def send_out(jp, ib):
         for k in range(per_blk):
             dst_row = ib * per_blk + k
 
@@ -256,13 +247,8 @@
             def _():
                 out_ref[me_r, jp] = outb[jp, my_rows, :]
 
-    units = cols * hj
-
-    def attend(t):
-        ib, jp = block_of(t // hj), t % hj
-        t_next = (t + 1) % units
-        ib_next, jp_next = block_of(t_next // hj), t_next % hj
-        finish_unit(jnp.maximum(t - 1, 0))
+    def attend(jp, ib, jp_prev, ib_prev, jp_next, ib_next):
+        finish_unit(jp_prev, ib_prev)
         for h in range(heads):
             nxt = (ib, jp, h + 2) if h + 2 < heads else (ib_next, jp_next, h + 2 - heads)
             s = scores_dot(*nxt)
@@ -270,7 +256,6 @@
             for c in range(halves):
                 mx = drain(s, c, nxt[2], mx)
                 l, o = weigh(jp, h, h, c, l, o)
-
             mm_s[nxt[2]] = jnp.max(mx, axis=0, keepdims=True)
             os_[h] = o
             lp[h] = l
@@ -283,46 +268,103 @@
     for h in range(2):
         scores(me_c, 0, h)
 
-    def first_unit(t, _):
+    def bring(blk):
+        d = (me_c - blk + cols) % cols
+        y_copy(d, blk).wait_recv()
+        f_copy(d, blk, mine).start()
+
+    def relay(side, blk, step):
+        part = pl.ds(core * hh + side * (hh // 2), hh // 2)
+        return remote(bias_ref.at[blk, part], bias_ref.at[blk, part], g_sem.at[0, side], g_sem.at[1, side], {'col': (me_c + step) % cols})
+
+    def brought(blk):
+        f_copy((me_c - blk + cols) % cols, blk, other).wait_recv()
+
+    def chain(units, prev, nxt):
+        seq = [prev] + units + [nxt]
+        for k in range(1, len(seq) - 1):
+            attend(*seq[k], *seq[k - 1], *seq[k + 1])
+
+    def pick(cond, yes, no):
+        return tuple(jnp.where(cond, y, n) for y, n in zip(yes, no))
+
+    n_a = hj // 2
+
+    def lead_in(t, _):
         wait_cols(t + 1)
         project(t + 1)
 
-        @pl.when(t > 1)
+        @pl.when(t == n_a - 1)
         def _():
-            send_out(t - 2)
-
-        attend(t)
+            bring(blk_a)
+            relay(0, blk_a, cols - 1).start()
+            bring(blk_b)
+            relay(1, blk_b, 1).start()
+
+        chain([(t, me_c)], (jnp.maximum(t - 1, 0), me_c), (t + 1, me_c))
         return 0
 
-    lax.fori_loop(0, hj - 1, first_unit, 0)
-
-    def unit(t, _):
-        for phase in range(1, cols):
-            @pl.when(t == phase * hj - 1)
-            def _():
-                blk = block_of(phase)
-                d = (me_c - blk + cols) % cols
-                f_copy(d, blk, other).wait_recv()
-
-            if phase + 1 < cols:
-                @pl.when(t == (phase + 1) * hj - 4)
-                def _():
-                    blk = block_of(phase + 1)
-                    d = (me_c - blk + cols) % cols
-                    y_copy(d, blk).wait_recv()
-                    f_copy(d, blk, mine).start()
-
-        send_out(t - 2)
-        attend(t)
+    lax.fori_loop(0, n_a, lead_in, 0)
+    brought(blk_a)
+    brought(blk_b)
+
+    def send_earlier(t):
+        @pl.when(t == n_a)
+        def _():
+            for k in range(n_a - 1):
+                send_out(k, me_c)
+
+        @pl.when(t > n_a)
+        def _():
+            send_out(*pick(t == n_a + 1, (n_a - 1, me_c), (t - n_a - 2, blk_b)))
+            send_out(t - 1, me_c)
+            send_out(t - n_a - 1, blk_a)
+
+    def three(t, _):
+        wait_cols(t + 1)
+        project(t + 1)
+        send_earlier(t)
+        chain([(t, me_c), (t - n_a, blk_a), (t - n_a, blk_b)], pick(t == n_a, (t - 1, me_c), (t - n_a - 1, blk_b)), (t + 1, me_c))
         return 0
 
-    blk = block_of(1)
-    y_copy((me_c - blk + cols) % cols, blk).wait_recv()
-    f_copy((me_c - blk + cols) % cols, blk, mine).start()
-    lax.fori_loop(hj - 1, units, unit, 0)
-    finish_unit(units - 1)
-    send_out(units - 2)
-    send_out(units - 1)
+    lax.fori_loop(n_a, hj - 1, three, 0)
+    relay(0, blk_d, cols - 1).wait_recv()
+    relay(1, blk_d, 1).wait_recv()
+    f_copy(2, blk_d, mine).start()
+
+    def bridge(t, _):
+        send_earlier(t)
+        chain([(t, me_c), (t - n_a, blk_a), (t - n_a, blk_b)], (t - n_a - 1, blk_b), (n_a, blk_a))
+        return 0
+
+    lax.fori_loop(hj - 1, hj, bridge, 0)
+    brought(blk_d)
+
+    def four(s, _):
+        @pl.when(s == 0)
+        def _():
+            send_out(n_a - 2, blk_b)
+            send_out(hj - 1, me_c)
+            send_out(n_a - 1, blk_a)
+
+        @pl.when(s > 0)
+        def _():
+            send_out(*pick(s == 1, (n_a - 1, blk_b), (2 * s - 3, blk_d)))
+            send_out(n_a - 1 + s, blk_a)
+            send_out(2 * s - 2, blk_d)
+            send_out(n_a - 1 + s, blk_b)
+
+        chain([(n_a + s, blk_a), (2 * s, blk_d), (n_a + s, blk_b), (2 * s + 1, blk_d)],
+              pick(s == 0, (n_a - 1, blk_b), (2 * s - 1, blk_d)), (jnp.minimum(n_a + 1 + s, hj - 1), blk_a))
+        return 0
+
+    lax.fori_loop(0, hj - n_a, four, 0)
+    send_out(hj - 3, blk_d)
+    send_out(hj - 1, blk_a)
+    send_out(hj - 2, blk_d)
+    send_out(hj - 1, blk_b)
+    finish_unit(hj - 1, blk_d)
+    send_out(hj - 1, blk_d)
 
     for d in order:
         x_copy(d, (me_r + d) % rows, me_r).wait_send()
@@ -330,6 +372,8 @@
             a_copy(d, jp, (me_r + d) % rows, me_r).wait_send()
     for d in y_order:
         y_copy(d, me_c).wait_send()
+    relay(0, blk_a, cols - 1).wait_send()
+    relay(1, blk_b, 1).wait_send()
     for d in range(cols):
         f_copy(d, me_c, mine).wait_send()
 
@@ -353,26 +397,13 @@
     wo = wo_ref[...].astype(F32)
     z = jnp.zeros((e, ch), F32)
     wo = tr(jnp.concatenate([blk for r in range(0, wo.shape[0], e) for blk in (wo[r:r + e], z)], 0))
-
-    def widen(t, _):
-        for jp in range(hj):
-            stage[pl.ds(pl.multiple_of((t * hj + jp) * pitch, 8), ti), :] = g_ref[t, jp].astype(F32)
-        return 0
-
-    lax.fori_loop(0, rows, widen, 0)
-
-    group = 8
-
-    def step(t, _):
-        for q in range(group):
-            i = t * group + q
-            x = stage[pl.ds(i, n_rj, stride=pitch), :]
-            y = pltpu.roll(x, lanes - e, 1)
-            x2 = jnp.concatenate([x.reshape(rows, 1, hj, lanes), y.reshape(rows, 1, hj, lanes)], 1).reshape(tj, lanes).astype(BF16)
-            out_ref[i] = (mm_nt(wo, x2) + z_ref[i].astype(F32)).astype(BF16)
-        return 0
-
-    lax.fori_loop(0, ti // group, step, 0)
+    for rj in range(n_rj):
+        stage[rj * pitch:rj * pitch + ti, :] = g_ref[rj // hj, rj % hj].astype(F32)
+    for i in range(ti):
+        x = stage[pl.ds(i, n_rj, stride=pitch), :]
+        y = pltpu.roll(x, lanes - e, 1)
+        x2 = jnp.concatenate([x.reshape(rows, 1, hj, lanes), y.reshape(rows, 1, hj, lanes)], 1).reshape(tj, lanes).astype(BF16)
+        out_ref[i] = (mm_nt(wo, x2) + z_ref[i].astype(F32)).astype(BF16)
 
 
 VM = pl.BlockSpec(memory_space=pltpu.VMEM)
@@ -411,17 +442,23 @@
                 pltpu.VMEM((heads, 8, 2 * tj), F32),
                 pltpu.VMEM((heads, 2 * e, 2 * tj), F32),
                 pltpu.VMEM((hj, n, 2 * proj), BF16),
-                dma((2, hj, rows)), dma((2, rows)), dma((2, cols)), dma((2, cols)), dma((2, rows)),
+                dma((2, hj, rows)), dma((2, rows)), dma((2, cols)), dma((2, cols)), dma((2, 2)), dma((2, rows)),
             ],
             compiler_params=pltpu.CompilerParams(collective_id=0, has_side_effects=True),
             name='triangle',
         )(z, ln_gamma.reshape(1, ch), ln_beta.reshape(1, ch), w_b.T, res_mask.reshape(1, n), w_q, w_k, w_v, w_g)
+        chunk = ti // 4
         out = pl.pallas_call(
             functools.partial(finish_kernel, proj // heads),
             out_shape=jax.ShapeDtypeStruct((ti, ch, tj), BF16),
-            in_specs=[VM] * 3,
-            out_specs=VM,
-            scratch_shapes=[pltpu.VMEM((rows * hj * (ti + PAD), 2 * ch), F32)],
+            grid=(ti // chunk,),
+            in_specs=[
+                pl.BlockSpec((rows, hj, chunk, 2 * ch), lambda i: (0, 0, i, 0)),
+                pl.BlockSpec((chunk, ch, tj), lambda i: (i, 0, 0)),
+                pl.BlockSpec((proj, ch), lambda i: (0, 0)),
+            ],
+            out_specs=pl.BlockSpec((chunk, ch, tj), lambda i: (i, 0, 0)),
+            scratch_shapes=[pltpu.VMEM((rows * hj * (chunk + PAD), 2 * ch), F32)],
             name='finish',
         )(back, z, w_o)
         return jnp.transpose(out, (0, 2, 1))

time: 58.2 us -> 53.6 us (0.921)
  the two profiles are of different devices: /device:TPU:97 before, /device:TPU:101 now
where the time goes in v5:
time: 53.6 us; the launch traced here: 53.5 us
  Pallas kernels  53.5 us (100%)
    pallas_call x1, Pallas kernels, body(): pl.pallas_call(functools.partial(triangle_kernel, rows, cols), out_shape=...  48.8 us
    pallas_call x1, Pallas kernels, body(): pl.pallas_call(functools.partial(finish_kernel, proj // heads), out_shape...  4.68 us

profile of v5, /device:TPU:101, one launch (start us, length us, event | category | flops | bytes accessed | tf_op | source)
XLA Modules:
  0.0 53.5 jit_solution(5228726635004850033)
XLA Ops:
  0.0 48.8 %triangle.1.g_ref = bf16[8,8,64,128]{3,2,1,0:T(8,128)(2,1)} custom-call(bf16[64,64,128]{2,1,0:T(8,128)(2,1)} %bitcast.6, f32[1,64]{1,0:T(1,128)} %bitcast.10, f32[1,64]{1,0:T(1,128)} %bitcast.11, bf16[4,64]{1,0:T(4,128)(2,1)} %bitcast.9, s32[1,512]{1,0:T(1,128)} %bitcast.8, bf16[64,64]{1,0:T(8,128)(2,1)} %wq_ref.1, bf16[64,64]{1,0:T(8,128)(2,1)} %wk_ref.1, ...), custom_call_target="tpu_custom_call" | custom-call | tf_op jit(solution)/shard_map/triangle/pallas_call | solution.py:424
  48.8 4.7 %finish.1 = bf16[64,64,128]{2,1,0:T(8,128)(2,1)} custom-call(bf16[8,8,64,128]{3,2,1,0:T(8,128)(2,1)} %triangle.1.g_ref, bf16[64,64,128]{2,1,0:T(8,128)(2,1)} %bitcast.7, bf16[64,64]{1,0:T(8,128)(2,1)} %wo_ref.1), custom_call_target="tpu_custom_call" | custom-call | tf_op jit(solution)/shard_map/finish/pallas_call | solution.py:451

commit v6 on v5

--- a/solution.py
+++ b/solution.py
@@ -54,7 +54,7 @@
 
 
 def triangle_kernel(rows, cols, z_ref, gamma_ref, beta_ref, wb_ref, mask_ref, wq_ref, wk_ref, wv_ref, wg_ref, out_ref,
-                    stage, bsc, bown, send, a_ref, bias_ref, qp, vt, gt, kh, ss, mm_s, lp, os_, outb, a_sem, x_sem, y_sem, f_sem, g_sem, o_sem):
+                    stage, bsc, bown, send, a_ref, bias_ref, qp, vt, gt, kh, ss, mm_s, lp, os_, outb, a_sem, x_sem, y_sem, f_sem, g_sem, o_sem, l_sem):
     ti, ch, tj = z_ref.shape
     heads = wb_ref.shape[0]
     hj, n, lanes = a_ref.shape
@@ -231,21 +231,17 @@
                 parts.append(gt[jp, ib, rs, :] * (os_[h, half * e:(half + 1) * e, ls] / l1[:, ls]))
         outb[jp, pl.ds(pl.multiple_of(ib * tj, tj), tj), :] = jnp.transpose(jnp.concatenate(parts, 0)).astype(BF16)
 
-    def out_copy(dst_row, src_jp, slot, slot_jp):
-        rs = pl.ds(pl.multiple_of(dst_row * ti, ti), ti)
-        return remote(outb.at[src_jp, rs, :], out_ref.at[slot, slot_jp], o_sem.at[0, dst_row], o_sem.at[1, slot], {'row': dst_row})
-
-    def send_out(jp, ib):
+    def out_copy(dst_row, jp, count):
+        rs, js = pl.ds(pl.multiple_of(dst_row * ti, ti), ti), pl.ds(jp, count)
+        return remote(outb.at[js, rs, :], out_ref.at[me_r, js], o_sem.at[0, dst_row], o_sem.at[1, me_r], {'row': dst_row})
+
+    def send_out(jp, ib, count=1):
         for k in range(per_blk):
             dst_row = ib * per_blk + k
 
             @pl.when(dst_row != me_r)
             def _():
-                out_copy(dst_row, jp, me_r, jp).start()
-
-            @pl.when(dst_row == me_r)
-            def _():
-                out_ref[me_r, jp] = outb[jp, my_rows, :]
+                out_copy(dst_row, jp, count).start()
 
     def attend(jp, ib, jp_prev, ib_prev, jp_next, ib_next):
         finish_unit(jp_prev, ib_prev)
@@ -308,23 +304,35 @@
     brought(blk_a)
     brought(blk_b)
 
+    def role(offsets):
+        return (me_c + sum(jnp.where(shift == k, o, 0) for k, o in enumerate(offsets))) % cols
+
+    shift = (chip - me_c + cols) % cols
+    odd = chip % 2
+    blk_p, blk_q, blk_r = role((1 + 2 * odd, 3, 1, 1)), role((2, 2, 3, 2)), role((3 - 2 * odd, 1, 2, 3))
+
+    def late(w):
+        own = shift == 0
+        jp = jnp.where(w < 0, w + hj, jnp.where(own, 2 * (w // 4) + w % 2, w % hj))
+        second = jnp.where(own, (w // 2) % 2, w // hj)
+        return jp, jnp.where(w < 0, blk_p, jnp.where(second == 0, blk_q, blk_r))
+
     def send_earlier(t):
-        @pl.when(t == n_a)
+        k = 2 * (t - n_a)
+
+        @pl.when(t == n_a + 1)
         def _():
-            for k in range(n_a - 1):
-                send_out(k, me_c)
-
-        @pl.when(t > n_a)
+            send_out(0, me_c, n_a)
+
+        @pl.when(t > n_a + 1)
         def _():
-            send_out(*pick(t == n_a + 1, (n_a - 1, me_c), (t - n_a - 2, blk_b)))
-            send_out(t - 1, me_c)
-            send_out(t - n_a - 1, blk_a)
+            send_out(k - 4, blk_p, 2)
 
     def three(t, _):
         wait_cols(t + 1)
         project(t + 1)
-        send_earlier(t)
-        chain([(t, me_c), (t - n_a, blk_a), (t - n_a, blk_b)], pick(t == n_a, (t - 1, me_c), (t - n_a - 1, blk_b)), (t + 1, me_c))
+        k = 2 * (t - n_a)
+        chain([(t, me_c), (k, blk_p), (k + 1, blk_p)], pick(t == n_a, (t - 1, me_c), (k - 1, blk_p)), (t + 1, me_c))
         return 0
 
     lax.fori_loop(n_a, hj - 1, three, 0)
@@ -333,38 +341,36 @@
     f_copy(2, blk_d, mine).start()
 
     def bridge(t, _):
-        send_earlier(t)
-        chain([(t, me_c), (t - n_a, blk_a), (t - n_a, blk_b)], (t - n_a - 1, blk_b), (n_a, blk_a))
+        send_out(0, me_c, n_a)
+        send_out(0, blk_p, n_a)
+        k = 2 * (t - n_a)
+        chain([(t, me_c), (k, blk_p), (k + 1, blk_p)], (k - 1, blk_p), (0, blk_q))
         return 0
 
+    brought(blk_d)
     lax.fori_loop(hj - 1, hj, bridge, 0)
-    brought(blk_d)
 
     def four(s, _):
         @pl.when(s == 0)
         def _():
-            send_out(n_a - 2, blk_b)
-            send_out(hj - 1, me_c)
-            send_out(n_a - 1, blk_a)
+            send_out(n_a, me_c, n_a)
+            send_out(hj - 4, blk_p, 2)
 
         @pl.when(s > 0)
         def _():
-            send_out(*pick(s == 1, (n_a - 1, blk_b), (2 * s - 3, blk_d)))
-            send_out(n_a - 1 + s, blk_a)
-            send_out(2 * s - 2, blk_d)
-            send_out(n_a - 1 + s, blk_b)
-
-        chain([(n_a + s, blk_a), (2 * s, blk_d), (n_a + s, blk_b), (2 * s + 1, blk_d)],
-              pick(s == 0, (n_a - 1, blk_b), (2 * s - 1, blk_d)), (jnp.minimum(n_a + 1 + s, hj - 1), blk_a))
+            send_out(*late(4 * s - 6), 2)
+            send_out(*late(4 * s - 4), 2)
+
+        chain([late(4 * s + k) for k in range(4)], late(4 * s - 1), late(jnp.minimum(4 * s + 4, 2 * hj - 1)))
         return 0
 
-    lax.fori_loop(0, hj - n_a, four, 0)
-    send_out(hj - 3, blk_d)
-    send_out(hj - 1, blk_a)
-    send_out(hj - 2, blk_d)
-    send_out(hj - 1, blk_b)
-    finish_unit(hj - 1, blk_d)
-    send_out(hj - 1, blk_d)
+    lax.fori_loop(0, hj // 2, four, 0)
+    send_out(*late(2 * hj - 6), 2)
+    send_out(*late(2 * hj - 4), 2)
+    finish_unit(*late(2 * hj - 1))
+    send_out(*late(2 * hj - 2), 2)
+    own = pltpu.make_async_copy(outb.at[:, my_rows, :], out_ref.at[me_r], l_sem)
+    own.start()
 
     for d in order:
         x_copy(d, (me_r + d) % rows, me_r).wait_send()
@@ -384,6 +390,7 @@
     for d in order:
         src = (me_r + rows - d) % rows
         all_out(src, src).wait_recv()
+    own.wait()
     for d in order:
         dst = (me_r + d) % rows
         all_out(dst, dst).wait_send()
@@ -425,7 +432,7 @@
             functools.partial(triangle_kernel, rows, cols),
             out_shape=jax.ShapeDtypeStruct((rows, hj, ti, 2 * ch), BF16),
             in_specs=[VM] * 9,
-            out_specs=VM,
+            out_specs=pl.BlockSpec(memory_space=pl.ANY),
             scratch_shapes=[
                 pltpu.VMEM((ti * (rows * hj + PAD), 2 * ch), F32),
                 pltpu.VMEM((ti * heads, tj), F32),
@@ -442,12 +449,12 @@
                 pltpu.VMEM((heads, 8, 2 * tj), F32),
                 pltpu.VMEM((heads, 2 * e, 2 * tj), F32),
                 pltpu.VMEM((hj, n, 2 * proj), BF16),
-                dma((2, hj, rows)), dma((2, rows)), dma((2, cols)), dma((2, cols)), dma((2, 2)), dma((2, rows)),
+                dma((2, hj, rows)), dma((2, rows)), dma((2, cols)), dma((2, cols)), dma((2, 2)), dma((2, rows)), dma,
             ],
             compiler_params=pltpu.CompilerParams(collective_id=0, has_side_effects=True),
             name='triangle',
         )(z, ln_gamma.reshape(1, ch), ln_beta.reshape(1, ch), w_b.T, res_mask.reshape(1, n), w_q, w_k, w_v, w_g)
-        chunk = ti // 4
+        chunk = ti // 2
         out = pl.pallas_call(
             functools.partial(finish_kernel, proj // heads),
             out_shape=jax.ShapeDtypeStruct((ti, ch, tj), BF16),

time: 53.6 us -> 51.6 us (0.963)
  the two profiles are of different devices: /device:TPU:101 before, /device:TPU:97 now
where the time goes in v6:
time: 51.6 us; the launch traced here: 51.5 us
  Pallas kernels  51.5 us (100%)
    pallas_call x1, Pallas kernels, body(): pl.pallas_call(functools.partial(triangle_kernel, rows, cols), out_shape=...  47.5 us
    pallas_call x1, Pallas kernels, body(): pl.pallas_call(functools.partial(finish_kernel, proj // heads), out_shape...  3.94 us

profile of v6, /device:TPU:97, one launch (start us, length us, event | category | flops | bytes accessed | tf_op | source)
XLA Modules:
  0.0 51.5 jit_solution(8146417562421995330)
XLA Ops:
  0.0 47.5 %triangle.1.g_ref = bf16[8,8,64,128]{3,2,1,0:T(8,128)(2,1)} custom-call(bf16[64,64,128]{2,1,0:T(8,128)(2,1)} %bitcast.6, f32[1,64]{1,0:T(1,128)} %bitcast.10, f32[1,64]{1,0:T(1,128)} %bitcast.11, bf16[4,64]{1,0:T(4,128)(2,1)} %bitcast.9, s32[1,512]{1,0:T(1,128)} %bitcast.8, bf16[64,64]{1,0:T(8,128)(2,1)} %wq_ref.1, bf16[64,64]{1,0:T(8,128)(2,1)} %wk_ref.1, ...), custom_call_target="tpu_custom_call" | custom-call | tf_op jit(solution)/shard_map/triangle/pallas_call | solution.py:431
  47.5 3.9 %finish.1 = bf16[64,64,128]{2,1,0:T(8,128)(2,1)} custom-call(bf16[8,8,64,128]{3,2,1,0:T(8,128)(2,1)} %triangle.1.g_ref, bf16[64,64,128]{2,1,0:T(8,128)(2,1)} %bitcast.7, bf16[64,64]{1,0:T(8,128)(2,1)} %wo_ref.1), custom_call_target="tpu_custom_call" | custom-call | tf_op jit(solution)/shard_map/finish/pallas_call | solution.py:458

commit v7 on v6

--- a/solution.py
+++ b/solution.py
@@ -84,7 +84,7 @@
     r_id = lax.broadcasted_iota(jnp.int32, wb16.shape, 0) // heads
     c_id = lax.broadcasted_iota(jnp.int32, wb16.shape, 1) // ch
     wb16 = jnp.where(r_id == c_id, wb16, 0.0).astype(BF16)
-    unroll = 4
+    unroll = 16
 
     def norm_step(t, _):
         for u in range(unroll):
@@ -406,11 +406,15 @@
     wo = tr(jnp.concatenate([blk for r in range(0, wo.shape[0], e) for blk in (wo[r:r + e], z)], 0))
     for rj in range(n_rj):
         stage[rj * pitch:rj * pitch + ti, :] = g_ref[rj // hj, rj % hj].astype(F32)
-    for i in range(ti):
+    def columns(i):
         x = stage[pl.ds(i, n_rj, stride=pitch), :]
         y = pltpu.roll(x, lanes - e, 1)
-        x2 = jnp.concatenate([x.reshape(rows, 1, hj, lanes), y.reshape(rows, 1, hj, lanes)], 1).reshape(tj, lanes).astype(BF16)
-        out_ref[i] = (mm_nt(wo, x2) + z_ref[i].astype(F32)).astype(BF16)
+        return jnp.concatenate([x.reshape(rows, 1, hj, lanes), y.reshape(rows, 1, hj, lanes)], 1).reshape(tj, lanes).astype(BF16)
+
+    for i in range(0, ti, 2):
+        r = mm_nt(wo, jnp.concatenate([columns(i), columns(i + 1)], 0))
+        out_ref[i] = (r[:, :tj] + z_ref[i].astype(F32)).astype(BF16)
+        out_ref[i + 1] = (r[:, tj:] + z_ref[i + 1].astype(F32)).astype(BF16)
 
 
 VM = pl.BlockSpec(memory_space=pltpu.VMEM)

time: 51.6 us -> 50.4 us (0.977)
  Pallas kernels: 51.5 us -> 50.2 us
    pallas_call x1, Pallas kernels: 3.94 us -> 3.3 us  [body(): pl.pallas_call(functools.partial(finish_kernel, proj // heads), out_shape...]
    pallas_call x1, Pallas kernels: 47.5 us -> 46.9 us  [body(): pl.pallas_call(functools.partial(triangle_kernel, rows, cols), out_shape=...]
where the time goes in v7:
time: 50.4 us; the launch traced here: 50.2 us
  Pallas kernels  50.2 us (100%)
    pallas_call x1, Pallas kernels, body(): pl.pallas_call(functools.partial(triangle_kernel, rows, cols), out_shape=...  46.9 us
    pallas_call x1, Pallas kernels, body(): pl.pallas_call(functools.partial(finish_kernel, proj // heads), out_shape...  3.3 us

profile of v7, /device:TPU:97, one launch (start us, length us, event | category | flops | bytes accessed | tf_op | source)
XLA Modules:
  0.0 50.2 jit_solution(17868847293354876878)
XLA Ops:
  0.0 46.9 %triangle.1.g_ref = bf16[8,8,64,128]{3,2,1,0:T(8,128)(2,1)} custom-call(bf16[64,64,128]{2,1,0:T(8,128)(2,1)} %bitcast.6, f32[1,64]{1,0:T(1,128)} %bitcast.10, f32[1,64]{1,0:T(1,128)} %bitcast.11, bf16[4,64]{1,0:T(4,128)(2,1)} %bitcast.9, s32[1,512]{1,0:T(1,128)} %bitcast.8, bf16[64,64]{1,0:T(8,128)(2,1)} %wq_ref.1, bf16[64,64]{1,0:T(8,128)(2,1)} %wk_ref.1, ...), custom_call_target="tpu_custom_call" | custom-call | tf_op jit(solution)/shard_map/triangle/pallas_call | solution.py:435
  46.9 3.3 %finish.1 = bf16[64,64,128]{2,1,0:T(8,128)(2,1)} custom-call(bf16[8,8,64,128]{3,2,1,0:T(8,128)(2,1)} %triangle.1.g_ref, bf16[64,64,128]{2,1,0:T(8,128)(2,1)} %bitcast.7, bf16[64,64]{1,0:T(8,128)(2,1)} %wo_ref.1), custom_call_target="tpu_custom_call" | custom-call | tf_op jit(solution)/shard_map/finish/pallas_call | solution.py:462

commit v8 on v7

--- a/solution.py
+++ b/solution.py
@@ -411,10 +411,10 @@
         y = pltpu.roll(x, lanes - e, 1)
         return jnp.concatenate([x.reshape(rows, 1, hj, lanes), y.reshape(rows, 1, hj, lanes)], 1).reshape(tj, lanes).astype(BF16)
 
-    for i in range(0, ti, 2):
-        r = mm_nt(wo, jnp.concatenate([columns(i), columns(i + 1)], 0))
-        out_ref[i] = (r[:, :tj] + z_ref[i].astype(F32)).astype(BF16)
-        out_ref[i + 1] = (r[:, tj:] + z_ref[i + 1].astype(F32)).astype(BF16)
+    for i in range(0, ti, 4):
+        r = mm_nt(wo, jnp.concatenate([columns(i + k) for k in range(4)], 0))
+        for k in range(4):
+            out_ref[i + k] = (r[:, k * tj:(k + 1) * tj] + z_ref[i + k].astype(F32)).astype(BF16)
 
 
 VM = pl.BlockSpec(memory_space=pltpu.VMEM)

time: 50.4 us -> 50.4 us (level)
  no operation moved by 1% of the time
where the time goes in v8:
time: 50.4 us; the launch traced here: 50.2 us
  Pallas kernels  50.2 us (100%)
    pallas_call x1, Pallas kernels, body(): pl.pallas_call(functools.partial(triangle_kernel, rows, cols), out_shape=...  46.9 us
    pallas_call x1, Pallas kernels, body(): pl.pallas_call(functools.partial(finish_kernel, proj // heads), out_shape...  3.3 us

profile of v8, /device:TPU:97, one launch (start us, length us, event | category | flops | bytes accessed | tf_op | source)
XLA Modules:
  0.0 50.2 jit_solution(17868847293354876878)
XLA Ops:
  0.0 46.9 %triangle.1.g_ref = bf16[8,8,64,128]{3,2,1,0:T(8,128)(2,1)} custom-call(bf16[64,64,128]{2,1,0:T(8,128)(2,1)} %bitcast.6, f32[1,64]{1,0:T(1,128)} %bitcast.10, f32[1,64]{1,0:T(1,128)} %bitcast.11, bf16[4,64]{1,0:T(4,128)(2,1)} %bitcast.9, s32[1,512]{1,0:T(1,128)} %bitcast.8, bf16[64,64]{1,0:T(8,128)(2,1)} %wq_ref.1, bf16[64,64]{1,0:T(8,128)(2,1)} %wk_ref.1, ...), custom_call_target="tpu_custom_call" | custom-call | tf_op jit(solution)/shard_map/triangle/pallas_call | solution.py:435
  46.9 3.3 %finish.1 = bf16[64,64,128]{2,1,0:T(8,128)(2,1)} custom-call(bf16[8,8,64,128]{3,2,1,0:T(8,128)(2,1)} %triangle.1.g_ref, bf16[64,64,128]{2,1,0:T(8,128)(2,1)} %bitcast.7, bf16[64,64]{1,0:T(8,128)(2,1)} %wo_ref.1), custom_call_target="tpu_custom_call" | custom-call | tf_op jit(solution)/shard_map/finish/pallas_call | solution.py:462
